TPU v7x, 128 devices: a whole 4x4x4 slice. The times are simulated.
128 devices in a mesh: fsdp: 16 (over z, y), model: 8 (over x, core).
Axes of the slice: x: 4, y: 4, z: 4, core: 2. Of those that a mesh axis runs over, the one named last changes fastest.
Arguments:
- x_in: bfloat16 [32, 512, 3072], P('fsdp', 'model')
- grad_out: bfloat16 [32, 512, 3072], P('fsdp', 'model')
- gain_attn: float32 [3072], replicated
- gain_mlp: float32 [3072], replicated
- w_qkv: bfloat16 [3072, 5120], P('fsdp', 'model')
- w_out: bfloat16 [3072, 3072], P('model', 'fsdp')
- w_gate: bfloat16 [3072, 8192], P('fsdp', 'model')
- w_up: bfloat16 [3072, 8192], P('fsdp', 'model')
- w_down: bfloat16 [8192, 3072], P('model', 'fsdp')
- rope_cos: float32 [512, 64], replicated
- rope_sin: float32 [512, 64], replicated
Outputs:
- output 1: bfloat16 [32, 512, 3072], P('fsdp', 'model')
- output 2: bfloat16 [32, 512, 3072], P('fsdp', 'model')
- output 3: float32 [3072], replicated
- output 4: float32 [3072], replicated
- output 5: float32 [3072, 5120], P('fsdp', 'model')
- output 6: float32 [3072, 3072], P('model', 'fsdp')
- output 7: float32 [3072, 8192], P('fsdp', 'model')
- output 8: float32 [3072, 8192], P('fsdp', 'model')
- output 9: float32 [8192, 3072], P('model', 'fsdp')
All inputs are finite; a program needn't handle non-finite values.
Results may differ from a plain program's by a relative error of at most 0.0161748.
Values are sent between devices in bfloat16 or wider.
A program may use at most 1 GiB of HBM per device.

v0:
```python
import jax
import jax.numpy as jnp
from jax import lax
from jax.sharding import PartitionSpec as P

NORM_EPS = 1e-5


def rms_scale(x_f32, gain):
    inv_rms = lax.rsqrt(jnp.mean(x_f32 * x_f32, axis=-1, keepdims=True) + NORM_EPS)
    return x_f32 * inv_rms * gain


def rotate(tensor, cos_t, sin_t):
    half = tensor.shape[-1] // 2
    first = tensor[..., :half]
    second = tensor[..., half:]
    return jnp.concatenate([first * cos_t - second * sin_t, second * cos_t + first * sin_t], axis=-1)


def rotate_back(cotangent, cos_t, sin_t):
    half = cotangent.shape[-1] // 2
    first = cotangent[..., :half]
    second = cotangent[..., half:]
    return jnp.concatenate([first * cos_t + second * sin_t, second * cos_t - first * sin_t], axis=-1)


def solution(mesh):
    fsdp_size = mesh.shape['fsdp']
    act_spec = P('fsdp', 'model', None)
    rows_spec = P('fsdp', 'model')
    cols_spec = P('model', 'fsdp')

    def gather_rows(w_shard):
        return lax.all_gather(w_shard, 'fsdp', axis=0, tiled=True)

    def gather_cols(w_shard):
        return lax.all_gather(w_shard, 'fsdp', axis=1, tiled=True)

    def gather_seq(tensor):
        return lax.all_gather(tensor, 'model', axis=1, tiled=True)

    def scatter_seq(tensor):
        return lax.psum_scatter(tensor, 'model', scatter_dimension=1, tiled=True)

    def device_fn(x_loc, dy_loc, gain_attn, gain_mlp, wqkv_sh, wout_sh, wgate_sh, wup_sh, wdown_sh, rope_cos, rope_sin):
        head_dim = 2 * rope_cos.shape[1]
        seq_full = rope_cos.shape[0]
        local_heads = wout_sh.shape[0] // head_dim
        local_kv = (wqkv_sh.shape[1] // head_dim - local_heads) // 2
        group_size = local_heads // local_kv
        micro_rows = x_loc.shape[0] // 2
        scale = head_dim ** -0.5
        pos_ids = jnp.arange(seq_full)
        causal = pos_ids[:, None] >= pos_ids[None, :]
        cos_q = rope_cos[:, None, None, :]
        sin_q = rope_sin[:, None, None, :]
        cos_k = rope_cos[:, None, :]
        sin_k = rope_sin[:, None, :]

        def micro_step(x_mb, dy_mb, accum):
            acc_gattn, acc_gmlp, acc_qkv, acc_out, acc_gate, acc_up, acc_down = accum
            x_f32 = x_mb.astype(jnp.float32)
            h_attn_f, norm_back_attn = jax.vjp(rms_scale, x_f32, gain_attn)
            h_attn = gather_seq(h_attn_f.astype(jnp.bfloat16))
            w_qkv = gather_rows(wqkv_sh)
            qkv = jnp.einsum('bsd,dc->bsc', h_attn, w_qkv, preferred_element_type=jnp.float32)
            qkv = qkv.reshape(micro_rows, seq_full, local_kv, group_size + 2, head_dim)
            query = rotate(qkv[:, :, :, :group_size], cos_q, sin_q).astype(jnp.bfloat16)
            key_rot = rotate(qkv[:, :, :, group_size], cos_k, sin_k).astype(jnp.bfloat16)
            value = qkv[:, :, :, group_size + 1].astype(jnp.bfloat16)
            scores = jnp.einsum('bqkgd,btkd->bkgqt', query, key_rot, preferred_element_type=jnp.float32) * scale
            attn_prob = jax.nn.softmax(jnp.where(causal, scores, -1e30), axis=-1)
            prob_bf = attn_prob.astype(jnp.bfloat16)
            attn = jnp.einsum('bkgqt,btkd->bqkgd', prob_bf, value, preferred_element_type=jnp.float32)
            attn_flat = attn.astype(jnp.bfloat16).reshape(micro_rows, seq_full, local_heads * head_dim)
            w_out = gather_cols(wout_sh)
            attn_red = scatter_seq(jnp.einsum('bsh,hd->bsd', attn_flat, w_out, preferred_element_type=jnp.float32))
            mid_f32 = (x_f32 + attn_red.astype(jnp.bfloat16).astype(jnp.float32)).astype(jnp.bfloat16).astype(jnp.float32)
            h_mlp_f, norm_back_mlp = jax.vjp(rms_scale, mid_f32, gain_mlp)
            h_mlp = gather_seq(h_mlp_f.astype(jnp.bfloat16))
            w_gate = gather_rows(wgate_sh)
            w_up = gather_rows(wup_sh)
            gate = jnp.einsum('bsd,df->bsf', h_mlp, w_gate, preferred_element_type=jnp.float32)
            up_proj = jnp.einsum('bsd,df->bsf', h_mlp, w_up, preferred_element_type=jnp.float32)
            sig_gate = jax.nn.sigmoid(gate)
            silu_gate = gate * sig_gate
            gated_act = (silu_gate * up_proj).astype(jnp.bfloat16)
            w_down = gather_cols(wdown_sh)
            mlp_red = scatter_seq(jnp.einsum('bsf,fd->bsd', gated_act, w_down, preferred_element_type=jnp.float32))
            y_mb = (mid_f32 + mlp_red.astype(jnp.bfloat16).astype(jnp.float32)).astype(jnp.bfloat16)

            dy_full = gather_seq(dy_mb)
            w_down_b = gather_cols(wdown_sh)
            d_act = jnp.einsum('bsd,fd->bsf', dy_full, w_down_b, preferred_element_type=jnp.float32).astype(jnp.bfloat16).astype(jnp.float32)
            acc_down = acc_down + jnp.einsum('bsf,bsd->fd', gated_act, dy_full, preferred_element_type=jnp.float32)
            d_gate = (d_act * up_proj * sig_gate * (1.0 + gate * (1.0 - sig_gate))).astype(jnp.bfloat16)
            d_up = (d_act * silu_gate).astype(jnp.bfloat16)
            w_gate_b = gather_rows(wgate_sh)
            w_up_b = gather_rows(wup_sh)
            dh_mlp = scatter_seq(jnp.einsum('bsf,df->bsd', d_gate, w_gate_b, preferred_element_type=jnp.float32)
                                 + jnp.einsum('bsf,df->bsd', d_up, w_up_b, preferred_element_type=jnp.float32))
            acc_gate = acc_gate + jnp.einsum('bsd,bsf->df', h_mlp, d_gate, preferred_element_type=jnp.float32)
            acc_up = acc_up + jnp.einsum('bsd,bsf->df', h_mlp, d_up, preferred_element_type=jnp.float32)
            d_mid_norm, d_gain_mlp = norm_back_mlp(dh_mlp.astype(jnp.bfloat16).astype(jnp.float32))
            d_mid = (dy_mb.astype(jnp.float32) + d_mid_norm).astype(jnp.bfloat16)

            d_mid_full = gather_seq(d_mid)
            w_out_b = gather_cols(wout_sh)
            d_attn = jnp.einsum('bsd,hd->bsh', d_mid_full, w_out_b, preferred_element_type=jnp.float32).astype(jnp.bfloat16)
            acc_out = acc_out + jnp.einsum('bsh,bsd->hd', attn_flat, d_mid_full, preferred_element_type=jnp.float32)
            d_attn = d_attn.reshape(micro_rows, seq_full, local_kv, group_size, head_dim)
            d_prob = jnp.einsum('bqkgd,btkd->bkgqt', d_attn, value, preferred_element_type=jnp.float32)
            d_value = jnp.einsum('bkgqt,bqkgd->btkd', prob_bf, d_attn, preferred_element_type=jnp.float32)
            row_dot = jnp.sum(d_prob * attn_prob, axis=-1, keepdims=True)
            d_scores = (attn_prob * (d_prob - row_dot) * scale).astype(jnp.bfloat16)
            d_query = jnp.einsum('bkgqt,btkd->bqkgd', d_scores, key_rot, preferred_element_type=jnp.float32)
            d_key = jnp.einsum('bkgqt,bqkgd->btkd', d_scores, query, preferred_element_type=jnp.float32)
            d_qkv = jnp.concatenate([rotate_back(d_query, cos_q, sin_q),
                                     rotate_back(d_key, cos_k, sin_k)[:, :, :, None],
                                     d_value[:, :, :, None]], axis=3)
            d_qkv = d_qkv.astype(jnp.bfloat16).reshape(micro_rows, seq_full, -1)
            w_qkv_b = gather_rows(wqkv_sh)
            dh_attn = scatter_seq(jnp.einsum('bsc,dc->bsd', d_qkv, w_qkv_b, preferred_element_type=jnp.float32))
            acc_qkv = acc_qkv + jnp.einsum('bsd,bsc->dc', h_attn, d_qkv, preferred_element_type=jnp.float32)
            d_x_norm, d_gain_attn = norm_back_attn(dh_attn.astype(jnp.bfloat16).astype(jnp.float32))
            dx_mb = (d_mid.astype(jnp.float32) + d_x_norm).astype(jnp.bfloat16)
            new_accum = (acc_gattn + d_gain_attn, acc_gmlp + d_gain_mlp, acc_qkv, acc_out, acc_gate, acc_up, acc_down)
            return y_mb, dx_mb, new_accum

        accum = (jnp.zeros_like(gain_attn), jnp.zeros_like(gain_mlp),
                 jnp.zeros((wqkv_sh.shape[0] * fsdp_size, wqkv_sh.shape[1]), jnp.float32),
                 jnp.zeros((wout_sh.shape[0], wout_sh.shape[1] * fsdp_size), jnp.float32),
                 jnp.zeros((wgate_sh.shape[0] * fsdp_size, wgate_sh.shape[1]), jnp.float32),
                 jnp.zeros((wup_sh.shape[0] * fsdp_size, wup_sh.shape[1]), jnp.float32),
                 jnp.zeros((wdown_sh.shape[0], wdown_sh.shape[1] * fsdp_size), jnp.float32))
        y_parts = []
        dx_parts = []
        for micro_idx in range(2):
            lo_row = micro_idx * micro_rows
            y_mb, dx_mb, accum = micro_step(x_loc[lo_row:lo_row + micro_rows], dy_loc[lo_row:lo_row + micro_rows], accum)
            y_parts.append(y_mb)
            dx_parts.append(dx_mb)
        gain_grads = lax.psum((accum[0], accum[1]), ('fsdp', 'model'))
        return (jnp.concatenate(y_parts, axis=0), jnp.concatenate(dx_parts, axis=0), gain_grads[0], gain_grads[1],
                lax.psum_scatter(accum[2], 'fsdp', scatter_dimension=0, tiled=True),
                lax.psum_scatter(accum[3], 'fsdp', scatter_dimension=1, tiled=True),
                lax.psum_scatter(accum[4], 'fsdp', scatter_dimension=0, tiled=True),
                lax.psum_scatter(accum[5], 'fsdp', scatter_dimension=0, tiled=True),
                lax.psum_scatter(accum[6], 'fsdp', scatter_dimension=1, tiled=True))

    in_specs = (act_spec, act_spec, P(), P(), rows_spec, cols_spec, rows_spec, rows_spec, cols_spec, P(), P())
    out_specs = (act_spec, act_spec, P(), P(), rows_spec, cols_spec, rows_spec, rows_spec, cols_spec)
    return jax.shard_map(device_fn, mesh=mesh, in_specs=in_specs, out_specs=out_specs, check_vma=False)
```

profile of v0, /device:TPU:1, one launch (start us, length us, event | category | flops | bytes accessed | tf_op | source)
XLA Modules:
  0.0 1435.7 jit_solution(12168490967807861720)
XLA Ops:
  14.2 48.9 %all-gather.16.cloned.1.call-done = bf16[3072,640]{1,0:T(8,128)(2,1)} async-done(((bf16[192,640]{1,0:T(8,128)(2,1)}), bf16[3072,640]{1,0:T(8,128)(2,1)}) %all-gather.16.cloned.1.call-update) | async-done | bytes 3932176 | tf_op jit(solution)/shard_map/all_gather | solution.py:35
  69.4 23.6 %all-gather.14.cloned.1.call-done = bf16[1,512,3072]{2,1,0:T(8,128)(2,1)} async-done(((bf16[1,64,3072]{2,1,0:T(8,128)(2,1)}), bf16[1,512,3072]{2,1,0:T(8,128)(2,1)}) %all-gather.14.cloned.1.call-update) | async-done | bytes 3145744 | tf_op jit(solution)/shard_map/all_gather | solution.py:41
  98.4 24.5 %all-gather.28.cloned.1.call-done = bf16[1,512,3072]{2,1,0:T(8,128)(2,1)} async-done(((bf16[1,64,3072]{2,1,0:T(8,128)(2,1)}), bf16[1,512,3072]{2,1,0:T(8,128)(2,1)}) %all-gather.28.cloned.1.call-update) | async-done | bytes 3145744 | tf_op jit(solution)/shard_map/all_gather | solution.py:41
  136.2 32.7 %all-gather.18.cloned.1.call-done = bf16[384,3072]{0,1:T(8,128)(2,1)} async-done(((bf16[384,192]{0,1:T(8,128)(2,1)}), bf16[384,3072]{0,1:T(8,128)(2,1)}) %all-gather.18.cloned.1.call-update) | async-done | bytes 2359312 | tf_op jit(solution)/shard_map/all_gather | solution.py:38
  187.3 30.8 %reduce-scatter.14.cloned.1.call-done = f32[1,64,3072]{2,1,0:T(8,128)} async-done(((f32[1,512,3072]{2,1,0:T(8,128)}), f32[1,64,3072]{2,1,0:T(8,128)}) %reduce-scatter.14.cloned.1.call-update) | async-done | bytes 786448 | tf_op jit(solution)/shard_map/reduce_scatter | solution.py:44
  218.1 44.5 %reduce-scatter.18.cloned.1.call-done = f32[1,64,3072]{2,1,0:T(8,128)} async-done(((f32[1,512,3072]{2,1,0:T(8,128)}), f32[1,64,3072]{2,1,0:T(8,128)}) %reduce-scatter.18.cloned.1.call-update) | async-done | bytes 786448 | tf_op jit(solution)/shard_map/reduce_scatter | solution.py:44
  266.1 26.8 %all-gather.32.cloned.1.call-done = bf16[1,512,3072]{2,1,0:T(8,128)(2,1)} async-done(((bf16[1,64,3072]{2,1,0:T(8,128)(2,1)}), bf16[1,512,3072]{2,1,0:T(8,128)(2,1)}) %all-gather.32.cloned.1.call-update) | async-done | bytes 3145744 | tf_op jit(solution)/shard_map/all_gather | solution.py:41
  292.9 62.7 %all-gather.26.cloned.1.call-done = bf16[1024,3072]{0,1:T(8,128)(2,1)} async-done(((bf16[1024,192]{0,1:T(8,128)(2,1)}), bf16[1024,3072]{0,1:T(8,128)(2,1)}) %all-gather.26.cloned.1.call-update) | async-done | bytes 6291472 | tf_op jit(solution)/shard_map/all_gather | solution.py:38
  363.8 54.6 %all-gather.22.cloned.1.call-done = bf16[3072,1024]{1,0:T(8,128)(2,1)} async-done(((bf16[192,1024]{1,0:T(8,128)(2,1)}), bf16[3072,1024]{1,0:T(8,128)(2,1)}) %all-gather.22.cloned.1.call-update) | async-done | bytes 6291472 | tf_op jit(solution)/shard_map/all_gather | solution.py:35
  418.3 29.8 %all-gather.20.cloned.1.call-done = bf16[1,512,3072]{2,1,0:T(8,128)(2,1)} async-done(((bf16[1,64,3072]{2,1,0:T(8,128)(2,1)}), bf16[1,512,3072]{2,1,0:T(8,128)(2,1)}) %all-gather.20.cloned.1.call-update) | async-done | bytes 3145744 | tf_op jit(solution)/shard_map/all_gather | solution.py:41
  448.1 8.5 fusion.37
  456.6 54.2 %all-gather.24.cloned.1.call-done = bf16[3072,1024]{1,0:T(8,128)(2,1)} async-done(((bf16[192,1024]{1,0:T(8,128)(2,1)}), bf16[3072,1024]{1,0:T(8,128)(2,1)}) %all-gather.24.cloned.1.call-update) | async-done | bytes 6291472 | tf_op jit(solution)/shard_map/all_gather | solution.py:35
  510.8 9.8 fusion.51
  524.6 16.7 %add_bitcast_fusion.1 = f32[1,512,3072]{2,1,0:T(8,128)} fusion(f32[512,3072]{1,0:T(8,128)S(1)} %fusion.188, bf16[3072,1024]{1,0:T(8,128)(2,1)S(1)} %copy-done.86, bf16[512,1024]{1,0:T(8,128)(2,1)S(1)} %copy-done.90, f32[512,1024]{1,0:T(8,128)S(1)} %copy-done.89), kind=kOutput, calls=%fused_computation.1 | convolution fusion | flops 3226468352 | bytes 22020096 | tf_op jit(solution)/shard_map/bsf,df->bsd/dot_general | solution.py:102
  542.2 41.2 %reduce-scatter.22.cloned.1.call-done = f32[1,64,3072]{2,1,0:T(8,128)} async-done(((f32[1,512,3072]{2,1,0:T(8,128)}), f32[1,64,3072]{2,1,0:T(8,128)}) %reduce-scatter.22.cloned.1.call-update) | async-done | bytes 786448 | tf_op jit(solution)/shard_map/reduce_scatter | solution.py:44
  586.3 27.4 %all-gather.36.cloned.1.call-done = bf16[1,512,3072]{2,1,0:T(8,128)(2,1)} async-done(((bf16[1,64,3072]{2,1,0:T(8,128)(2,1)}), bf16[1,512,3072]{2,1,0:T(8,128)(2,1)}) %all-gather.36.cloned.1.call-update) | async-done | bytes 3145744 | tf_op jit(solution)/shard_map/all_gather | solution.py:41
  621.9 21.5 %all-gather.30.cloned.1.call-done = bf16[1,512,3072]{2,1,0:T(8,128)(2,1)} async-done(((bf16[1,64,3072]{2,1,0:T(8,128)(2,1)}), bf16[1,512,3072]{2,1,0:T(8,128)(2,1)}) %all-gather.30.cloned.1.call-update) | async-done | bytes 3145744 | tf_op jit(solution)/shard_map/all_gather | solution.py:41
  650.1 8.6 fusion.55
  668.8 9.2 convolution_bitcast_fusion.4
  678.4 9.2 convolution_bitcast_fusion.2
  688.9 21.8 %reduce-scatter.26.cloned.1.call-done = f32[1,64,3072]{2,1,0:T(8,128)} async-done(((f32[1,512,3072]{2,1,0:T(8,128)}), f32[1,64,3072]{2,1,0:T(8,128)}) %reduce-scatter.26.cloned.1.call-update) | async-done | bytes 786448 | tf_op jit(solution)/shard_map/reduce_scatter | solution.py:44
  714.0 41.2 %reduce-scatter.16.cloned.1.call-done = f32[1,64,3072]{2,1,0:T(8,128)} async-done(((f32[1,512,3072]{2,1,0:T(8,128)}), f32[1,64,3072]{2,1,0:T(8,128)}) %reduce-scatter.16.cloned.1.call-update) | async-done | bytes 786448 | tf_op jit(solution)/shard_map/reduce_scatter | solution.py:44
  755.2 44.5 %reduce-scatter.20.cloned.1.call-done = f32[1,64,3072]{2,1,0:T(8,128)} async-done(((f32[1,512,3072]{2,1,0:T(8,128)}), f32[1,64,3072]{2,1,0:T(8,128)}) %reduce-scatter.20.cloned.1.call-update) | async-done | bytes 786448 | tf_op jit(solution)/shard_map/reduce_scatter | solution.py:44
  804.4 27.4 %all-gather.38.cloned.1.call-done = bf16[1,512,3072]{2,1,0:T(8,128)(2,1)} async-done(((bf16[1,64,3072]{2,1,0:T(8,128)(2,1)}), bf16[1,512,3072]{2,1,0:T(8,128)(2,1)}) %all-gather.38.cloned.1.call-update) | async-done | bytes 3145744 | tf_op jit(solution)/shard_map/all_gather | solution.py:41
  841.0 20.1 %all-gather.34.cloned.1.call-done = bf16[1,512,3072]{2,1,0:T(8,128)(2,1)} async-done(((bf16[1,64,3072]{2,1,0:T(8,128)(2,1)}), bf16[1,512,3072]{2,1,0:T(8,128)(2,1)}) %all-gather.34.cloned.1.call-update) | async-done | bytes 3145744 | tf_op jit(solution)/shard_map/all_gather | solution.py:41
  951.3 16.6 %reduce-scatter.24.cloned.1.call-done = f32[1,64,3072]{2,1,0:T(8,128)} async-done(((f32[1,512,3072]{2,1,0:T(8,128)}), f32[1,64,3072]{2,1,0:T(8,128)}) %reduce-scatter.24.cloned.1.call-update) | async-done | bytes 786448 | tf_op jit(solution)/shard_map/reduce_scatter | solution.py:44
  969.8 68.5 %all-reduce = (f32[3072]{0:T(1024)}, f32[3072]{0:T(1024)}) all-reduce(f32[3072]{0:T(1024)S(1)} %add.199, f32[3072]{0:T(1024)S(1)} %add.200), channel_id=1, replica_groups=mesh['fsdp'=16,'model'=8] {'fsdp','model'}, use_global_device_ids=true, to_apply=%region_24.25 | all-reduce | flops 6144 | bytes 49152 | tf_op jit(solution)/shard_map/psum | solution.py:144
  1041.2 24.8 %reduce-scatter.38.cloned.1.call-done = f32[1024,192]{0,1:T(8,128)} async-done(((f32[1024,3072]{0,1:T(8,128)}), f32[1024,192]{0,1:T(8,128)}) %reduce-scatter.38.cloned.1.call-update) | async-done | bytes 786448 | tf_op jit(solution)/shard_map/reduce_scatter | solution.py:150
  1066.0 97.0 %reduce-scatter.36.cloned.1.call-done = f32[192,1024]{1,0:T(8,128)} async-done(((f32[3072,1024]{1,0:T(8,128)}), f32[192,1024]{1,0:T(8,128)}) %reduce-scatter.36.cloned.1.call-update) | async-done | bytes 786448 | tf_op jit(solution)/shard_map/reduce_scatter | solution.py:149
  1163.0 97.0 %reduce-scatter.34.cloned.1.call-done = f32[192,1024]{1,0:T(8,128)} async-done(((f32[3072,1024]{1,0:T(8,128)}), f32[192,1024]{1,0:T(8,128)}) %reduce-scatter.34.cloned.1.call-update) | async-done | bytes 786448 | tf_op jit(solution)/shard_map/reduce_scatter | solution.py:148
  1260.0 81.2 %reduce-scatter.32.cloned.1.call-done = f32[384,192]{0,1:T(8,128)} async-done(((f32[384,3072]{0,1:T(8,128)}), f32[384,192]{0,1:T(8,128)}) %reduce-scatter.32.cloned.1.call-update) | async-done | bytes 294928 | tf_op jit(solution)/shard_map/reduce_scatter | solution.py:147
  1341.3 87.5 %reduce-scatter.30.cloned.1.call-done = f32[192,640]{1,0:T(8,128)} async-done(((f32[3072,640]{1,0:T(8,128)}), f32[192,640]{1,0:T(8,128)}) %reduce-scatter.30.cloned.1.call-update) | async-done | bytes 491536 | tf_op jit(solution)/shard_map/reduce_scatter | solution.py:146
  (316 shorter events, 207.0 us)
Async XLA Ops:
  7.2 56.0 %all-gather.16.cloned.1.call-start = ((), (), s32[]{:S(2)}) async-start(), calls=%async_computation.14 | async-start | bytes 4177920 | tf_op jit(solution)/shard_map/all_gather | solution.py:35
  7.9 85.2 %all-gather.14.cloned.1.call-start = ((), (), s32[]{:S(2)}) async-start(), calls=%async_computation.13 | async-start | bytes 3538944 | tf_op jit(solution)/shard_map/all_gather | solution.py:41
  12.8 110.2 %all-gather.28.cloned.1.call-start = ((), (), s32[]{:S(2)}) async-start(), calls=%async_computation.22 | async-start | bytes 3538944 | tf_op jit(solution)/shard_map/all_gather | solution.py:41
  13.5 155.4 %all-gather.18.cloned.1.call-start = ((), (), s32[]{:S(2)}) async-start(), calls=%async_computation.15 | async-start | bytes 2506752 | tf_op jit(solution)/shard_map/all_gather | solution.py:38
  14.1 204.0 %reduce-scatter.14.cloned.1.call-start = ((), (), s32[]{:S(2)}) async-start(), calls=%async_computation.16 | async-start | bytes 7077888 | tf_op jit(solution)/shard_map/reduce_scatter | solution.py:44
  14.2 162.0 %copy-start.23 = (pred[512,512]{0,1:T(8,128)(4,1)}, pred[512,512]{0,1:T(8,128)(4,1)S(1)}, u32[]{:S(2)}) copy-start(pred[512,512]{0,1:T(8,128)(4,1)S(1)} %iota_compare_fusion) | copy-start | bytes 786436
  175.2 87.5 %reduce-scatter.18.cloned.1.call-start = ((), (), s32[]{:S(2)}) async-start(), calls=%async_computation.23 | async-start | bytes 7077888 | tf_op jit(solution)/shard_map/reduce_scatter | solution.py:44
  183.8 109.2 %all-gather.32.cloned.1.call-start = ((), (), s32[]{:S(2)}) async-start(), calls=%async_computation.26 | async-start | bytes 3538944 | tf_op jit(solution)/shard_map/all_gather | solution.py:41
  185.8 169.8 %all-gather.26.cloned.1.call-start = ((), (), s32[]{:S(2)}) async-start(), calls=%async_computation.20 | async-start | bytes 6684672 | tf_op jit(solution)/shard_map/all_gather | solution.py:38
  186.6 231.8 %all-gather.22.cloned.1.call-start = ((), (), s32[]{:S(2)}) async-start(), calls=%async_computation.18 | async-start | bytes 6684672 | tf_op jit(solution)/shard_map/all_gather | solution.py:35
  187.3 260.9 %all-gather.20.cloned.1.call-start = ((), (), s32[]{:S(2)}) async-start(), calls=%async_computation.17 | async-start | bytes 3538944 | tf_op jit(solution)/shard_map/all_gather | solution.py:41
  264.4 99.4 %copy-start.84 = (f32[64]{0:T(128)}, f32[64]{0:T(128)S(1)}, u32[]{:S(2)}) copy-start(f32[64]{0:T(128)S(1)} %get-tuple-element.27) | copy-start | bytes 772
  264.4 277.8 %copy-start.83 = (f32[64]{0:T(128)}, f32[64]{0:T(128)S(1)}, u32[]{:S(2)}) copy-start(f32[64]{0:T(128)S(1)} %get-tuple-element.51) | copy-start | bytes 772
  264.4 319.0 %copy-start.9 = (bf16[1,64,3072]{2,1,0:T(8,128)(2,1)}, bf16[1,64,3072]{2,1,0:T(8,128)(2,1)S(1)}, u32[]{:S(2)}) copy-start(bf16[1,64,3072]{2,1,0:T(8,128)(2,1)S(1)} %get-tuple-element.52) | copy-start | bytes 1179652
  264.4 319.0 %copy-start.78 = (f32[64]{0:T(128)}, f32[64]{0:T(128)S(1)}, u32[]{:S(2)}) copy-start(f32[64]{0:T(128)S(1)} %fusion.168) | copy-start | bytes 772
  265.4 245.5 %all-gather.24.cloned.1.call-start = ((), (), s32[]{:S(2)}) async-start(), calls=%async_computation.19 | async-start | bytes 6684672 | tf_op jit(solution)/shard_map/all_gather | solution.py:35
  266.1 317.3 %reduce-scatter.22.cloned.1.call-start = ((), (), s32[]{:S(2)}) async-start(), calls=%async_computation.27 | async-start | bytes 7077888 | tf_op jit(solution)/shard_map/reduce_scatter | solution.py:44
  541.4 72.3 %all-gather.36.cloned.1.call-start = ((), (), s32[]{:S(2)}) async-start(), calls=%async_computation.30 | async-start | bytes 3538944 | tf_op jit(solution)/shard_map/all_gather | solution.py:41
  542.1 101.3 %all-gather.30.cloned.1.call-start = ((), (), s32[]{:S(2)}) async-start(), calls=%async_computation.24 | async-start | bytes 3538944 | tf_op jit(solution)/shard_map/all_gather | solution.py:41
  586.2 124.5 %reduce-scatter.26.cloned.1.call-start = ((), (), s32[]{:S(2)}) async-start(), calls=%async_computation.31 | async-start | bytes 7077888 | tf_op jit(solution)/shard_map/reduce_scatter | solution.py:44
  668.7 86.5 %reduce-scatter.16.cloned.1.call-start = ((), (), s32[]{:S(2)}) async-start(), calls=%async_computation.21 | async-start | bytes 7077888 | tf_op jit(solution)/shard_map/reduce_scatter | solution.py:44
  678.0 121.7 %reduce-scatter.20.cloned.1.call-start = ((), (), s32[]{:S(2)}) async-start(), calls=%async_computation.25 | async-start | bytes 7077888 | tf_op jit(solution)/shard_map/reduce_scatter | solution.py:44
  687.7 144.1 %all-gather.38.cloned.1.call-start = ((), (), s32[]{:S(2)}) async-start(), calls=%async_computation.32 | async-start | bytes 3538944 | tf_op jit(solution)/shard_map/all_gather | solution.py:41
  803.6 57.5 %all-gather.34.cloned.1.call-start = ((), (), s32[]{:S(2)}) async-start(), calls=%async_computation.28 | async-start | bytes 3538944 | tf_op jit(solution)/shard_map/all_gather | solution.py:41
  804.4 146.9 %reduce-scatter.28.cloned.1.call-start = ((), (), s32[]{:S(2)}) async-start(), calls=%async_computation.33 | async-start | bytes 7077888 | tf_op jit(solution)/shard_map/reduce_scatter | solution.py:44
  881.2 86.6 %reduce-scatter.24.cloned.1.call-start = ((), (), s32[]{:S(2)}) async-start(), calls=%async_computation.29 | async-start | bytes 7077888 | tf_op jit(solution)/shard_map/reduce_scatter | solution.py:44
  890.0 175.9 %reduce-scatter.38.cloned.1.call-start = ((), (), s32[]{:S(2)}) async-start(), calls=%async_computation.38 | async-start | bytes 13369344 | tf_op jit(solution)/shard_map/reduce_scatter | solution.py:150
  903.1 259.9 %reduce-scatter.36.cloned.1.call-start = ((), (), s32[]{:S(2)}) async-start(), calls=%async_computation.37 | async-start | bytes 13369344 | tf_op jit(solution)/shard_map/reduce_scatter | solution.py:149
  916.9 343.2 %reduce-scatter.34.cloned.1.call-start = ((), (), s32[]{:S(2)}) async-start(), calls=%async_computation.36 | async-start | bytes 13369344 | tf_op jit(solution)/shard_map/reduce_scatter | solution.py:148
  929.4 411.9 %reduce-scatter.32.cloned.1.call-start = ((), (), s32[]{:S(2)}) async-start(), calls=%async_computation.35 | async-start | bytes 5013504 | tf_op jit(solution)/shard_map/reduce_scatter | solution.py:147
  938.4 490.4 %reduce-scatter.30.cloned.1.call-start = ((), (), s32[]{:S(2)}) async-start(), calls=%async_computation.34 | async-start | bytes 8355840 | tf_op jit(solution)/shard_map/reduce_scatter | solution.py:146
  949.3 89.1 %copy-start.80 = (f32[64]{0:T(128)S(1)}, f32[64]{0:T(128)}, u32[]{:S(2)}) copy-start(f32[64]{0:T(128)} %copy-done.79) | copy-start | bytes 772
  (89 other events, 991.0 us)
Sparse Core Ops, SparseCore 0:
  10.1 52.9 all-gather.15
  65.4 27.6 all-gather.13
  95.3 27.5 all-gather.27
  124.9 43.9 all-gather.17
  175.3 42.7 reduce-scatter.13
  220.4 42.2 reduce-scatter.17
  264.9 27.9 all-gather.31
  295.1 60.4 all-gather.25
  357.7 60.5 all-gather.21
  420.5 27.6 all-gather.19
  450.3 60.4 all-gather.23
  541.5 41.8 reduce-scatter.21
  585.7 27.9 all-gather.35
  615.8 27.5 all-gather.29
  668.9 41.7 reduce-scatter.25
  713.0 42.1 reduce-scatter.15
  757.5 42.2 reduce-scatter.19
  803.8 28.0 all-gather.37
  833.5 27.5 all-gather.33
  881.4 41.7 reduce-scatter.27
  925.6 42.2 reduce-scatter.23
  971.9 94.0 reduce-scatter.37
  1070.0 92.9 reduce-scatter.35
  1166.9 93.1 reduce-scatter.33
  1264.0 77.2 reduce-scatter.31
  1345.2 83.4 reduce-scatter.29
where the time goes:
time: 1440 us
  waiting for transfers between devices  1090 us (76%)
  matrix products  212 us (15%)
  blocking collectives  68.5 us (5%)
  other arithmetic  29.2 us (2%)
  local copies, waits for them, and re-layouts  19.5 us (1%)
  between operations  15.9 us (1%)
    reduce_scatter x8, waiting for transfers between devices, scatter_seq(): return lax.psum_scatter(tensor, 'model', scatter_dimension=1, tiled=True)  241 us
    all_gather x8, waiting for transfers between devices, gather_seq(): return lax.all_gather(tensor, 'model', axis=1, tiled=True)  201 us
    all_gather x3, waiting for transfers between devices, gather_rows(): return lax.all_gather(w_shard, 'fsdp', axis=0, tiled=True)  158 us
    reduce_scatter x1, waiting for transfers between devices, device_fn(): lax.psum_scatter(accum[4], 'fsdp', scatter_dimension=0, tiled=True)  97 us
    reduce_scatter x1, waiting for transfers between devices, device_fn(): lax.psum_scatter(accum[5], 'fsdp', scatter_dimension=0, tiled=True)  97 us
    all_gather x2, waiting for transfers between devices, gather_cols(): return lax.all_gather(w_shard, 'fsdp', axis=1, tiled=True)  95.4 us
    reduce_scatter x1, waiting for transfers between devices, device_fn(): lax.psum_scatter(accum[2], 'fsdp', scatter_dimension=0, tiled=True)  87.5 us
    reduce_scatter x1, waiting for transfers between devices, device_fn(): lax.psum_scatter(accum[3], 'fsdp', scatter_dimension=1, tiled=True)  81.2 us
  transfers between devices with their start and end apart: 26, of which 25 were waited for; matrix products, arithmetic and copies ran while one was open for 12% of the time, Pallas kernels for 0%

commit v1 on v0

v1 whole, which is shorter than its diff:
```python
import functools

import jax
import jax.numpy as jnp
from jax import lax
from jax.experimental import pallas as pl
from jax.experimental.pallas import tpu as pltpu
from jax.sharding import PartitionSpec as P


NORM_EPS = 1e-5
F32 = jnp.float32
BF16 = jnp.bfloat16
MESH = pl.DeviceIdType.MESH
X_CHIPS = 4
ROWS = 16


def model_peers():
    m = lax.axis_index('model')
    x, c = m // 2, m % 2
    other = 2 * x + (1 - c)
    nxt = 2 * ((x + 1) % X_CHIPS) + c
    prv = 2 * ((x + 3) % X_CHIPS) + c
    return x, c, other, nxt, prv


def model_barrier(peers):
    sem = pltpu.get_barrier_semaphore()
    for peer in peers:
        pl.semaphore_signal(sem, inc=1, device_id={'model': peer}, device_id_type=MESH)
    pl.semaphore_wait(sem, len(peers))


def remote(src, dst, send_sem, recv_sem, peer):
    return pltpu.make_async_remote_copy(src_ref=src, dst_ref=dst, send_sem=send_sem, recv_sem=recv_sem,
                                        device_id={'model': peer}, device_id_type=MESH)


def row_loop(n_rows, fn):
    def step(i, carry):
        fn(pl.ds(pl.multiple_of(i * ROWS, ROWS), ROWS))
        return carry

    lax.fori_loop(0, n_rows // ROWS, step, 0)


class Gather:
    SEMS = 9

    def __init__(self, src, out, send, recv, local):
        self.src, self.out, self.send, self.recv, self.local = src, out, send, recv, local
        self.x, self.c, self.other, self.nxt, self.prv = model_peers()
        self.half = src.shape[0] // 2

    def slot(self, dx, core):
        return self.out.at[2 * ((self.x + dx) % X_CHIPS) + core]

    def part(self, dx, core, upper):
        return self.out.at[2 * ((self.x + dx) % X_CHIPS) + core, pl.ds(self.half * upper, self.half)]

    def copy(self, i, src, dst, peer):
        return remote(src, dst, self.send.at[i], self.recv.at[i], peer)

    def copies(self):
        c = self.c
        mine = self.slot(0, c)
        return [
            (self.src, mine, self.other), (self.src, mine, self.nxt), (self.src, mine, self.prv),
            (self.part(3, c, 0), self.part(3, c, 0), self.nxt), (self.part(1, c, 1), self.part(1, c, 1), self.prv),
            (self.slot(3, c), self.slot(3, c), self.other), (self.slot(1, c), self.slot(1, c), self.other),
            (self.part(2, c, 0), self.part(2, c, 0), self.other), (self.part(2, c, 1), self.part(2, c, 1), self.other),
        ]

    def landing(self):
        c, o = self.c, 1 - self.c
        return [self.slot(0, o), self.slot(3, c), self.slot(1, c), self.part(2, c, 0), self.part(2, c, 1),
                self.slot(3, o), self.slot(1, o), self.part(2, o, 0), self.part(2, o, 1)]

    def start(self, *which):
        table = self.copies()
        for i in which:
            self.copy(i, *table[i]).start()

    def wait_recv(self, *which):
        table = self.landing()
        for i in which:
            self.copy(i, table[i], table[i], self.other).wait_recv()

    def begin(self):
        pltpu.make_async_copy(self.src, self.slot(0, self.c), self.local).start()
        self.start(1, 2, 0)

    def forward_near(self):
        self.wait_recv(1)
        self.start(3, 5)
        self.wait_recv(2)
        self.start(4, 6)

    def forward_far(self):
        self.wait_recv(3)
        self.start(7)
        self.wait_recv(4)
        self.start(8)

    def finish(self):
        self.wait_recv(0, 5, 6, 7, 8)
        table = self.copies()
        for i in range(self.SEMS):
            self.copy(i, *table[i]).wait_send()
        pltpu.make_async_copy(self.src, self.slot(0, self.c), self.local).wait()


class RingGather:
    SEMS = 4

    def __init__(self, src, slot, nxt, prv, send, recv):
        self.src, self.slot, self.nxt, self.prv, self.send, self.recv = src, slot, nxt, prv, send, recv
        half = src.shape[0] // 2
        self.upper, self.lower = pl.ds(0, half), pl.ds(half, half)

    def copy(self, i, src, dst, peer):
        return pltpu.make_async_remote_copy(src_ref=src, dst_ref=dst, send_sem=self.send.at[i], recv_sem=self.recv.at[i],
                                            device_id={'fsdp': peer}, device_id_type=MESH)

    def copies(self):
        up, low = self.slot(3).at[self.upper], self.slot(1).at[self.lower]
        return [(self.src, self.slot(0), self.nxt), (self.src, self.slot(0), self.prv),
                (up, up, self.nxt), (low, low, self.prv)]

    def start(self, *which):
        table = self.copies()
        for i in which:
            self.copy(i, *table[i]).start()

    def wait_recv(self, *which):
        table = [self.slot(3), self.slot(1), self.slot(2).at[self.upper], self.slot(2).at[self.lower]]
        for i in which:
            self.copy(i, table[i], table[i], self.nxt).wait_recv()

    def near(self):
        self.wait_recv(0)
        self.start(2)
        self.wait_recv(1)
        self.start(3)

    def wait_send(self):
        table = self.copies()
        for i in range(self.SEMS):
            self.copy(i, *table[i]).wait_send()


class WeightGather:
    SEMS = 10

    def __init__(self, src, out, send, recv, local):
        self.src, self.out, self.local = src, out, local
        f = lax.axis_index('fsdp')
        z, y = f // 4, f % 4
        self.f = f
        rows = src.shape[0] // 2
        self.nxt = {'z': 4 * ((z + 1) % 4) + y, 'y': 4 * z + (y + 1) % 4}
        self.prv = {'z': 4 * ((z + 3) % 4) + y, 'y': 4 * z + (y + 3) % 4}
        self.first, self.second = [], []
        for color, (one, two) in enumerate((('y', 'z'), ('z', 'y'))):
            part = pl.ds(color * rows, rows)

            def at(d_one, d_two, one=one, part=part):
                dy, dz = (d_one, d_two) if one == 'y' else (d_two, d_one)
                return out.at[4 * ((z + dz) % 4) + (y + dy) % 4, part]

            base = 5 * color

            def ring(i, src_ref, slot, axis, base=base):
                return RingGather(src_ref, slot, self.nxt[axis], self.prv[axis], send.at[base + i], recv.at[base + i])

            self.first.append(ring(0, src.at[part], lambda d, at=at: at(d, 0), one))
            self.second.append([ring(1 + d, src.at[part] if d == 0 else at(d, 0),
                                     lambda e, d=d, at=at: at(d, e), two) for d in range(4)])

    def barrier_peers(self):
        return [self.nxt['z'], self.prv['z'], self.nxt['y'], self.prv['y']]

    def begin(self):
        pltpu.make_async_copy(self.src, self.out.at[self.f], self.local).start()
        for color in range(2):
            self.first[color].start(0, 1)
        for color in range(2):
            self.second[color][0].start(0, 1)

    def step_near(self):
        for color in range(2):
            one, two = self.first[color], self.second[color]
            one.wait_recv(0)
            one.start(2)
            two[3].start(0, 1)
        for color in range(2):
            one, two = self.first[color], self.second[color]
            one.wait_recv(1)
            one.start(3)
            two[1].start(0, 1)

    def step_own(self):
        for color in range(2):
            self.second[color][0].near()

    def step_far(self):
        for color in range(2):
            self.first[color].wait_recv(2, 3)
            self.second[color][2].start(0, 1)

    def step_second(self, d):
        for color in range(2):
            self.second[color][d].near()

    def finish(self):
        for color in range(2):
            for ring in self.second[color]:
                ring.wait_recv(2, 3)
            for ring in [self.first[color]] + self.second[color]:
                ring.wait_send()
        pltpu.make_async_copy(self.src, self.out.at[self.f], self.local).wait()


class Scatter:
    SEMS = 10
    DIST = (2, 1, 3, 0)
    CHUNKS = 4

    def __init__(self, rows_of, weight, box, pair, mine, far, near, send, recv):
        self.rows_of, self.weight, self.box = rows_of, weight, box
        self.pair, self.mine, self.far, self.near = pair, mine, far, near
        self.send, self.recv = send, recv
        self.x, self.c, self.other, self.nxt, self.prv = model_peers()
        self.rows, self.width = mine.shape[1], mine.shape[2]
        self.lo = pl.ds(0, self.width // 2)
        self.hi = pl.ds(self.width // 2, self.width // 2)

    def copies(self):
        rows = slice(None)
        m = self.mine
        return [(self.box.at[k], self.pair.at[k], self.other) for k in range(4)] + [
            (m.at[0, rows, self.lo], self.far.at[0], self.nxt), (m.at[0, rows, self.hi], self.far.at[1], self.prv),
            (m.at[1, rows, self.hi], self.near.at[0, rows, self.hi], self.nxt),
            (m.at[2, rows, self.lo], self.near.at[1, rows, self.lo], self.prv),
            (m.at[1, rows, self.lo], self.near.at[0, rows, self.lo], self.nxt),
            (m.at[2, rows, self.hi], self.near.at[1, rows, self.hi], self.prv),
        ]

    def copy(self, i):
        src, dst, peer = self.copies()[i]
        return remote(src, dst, self.send.at[i], self.recv.at[i], peer)

    def wait_recv(self, i):
        dst = self.copies()[i][1]
        remote(dst, dst, self.send.at[i], self.recv.at[i], self.other).wait_recv()

    def produce(self, k):
        place = 2 * ((self.x + self.DIST[k]) % X_CHIPS)
        left = jnp.concatenate([self.rows_of(place + self.c), self.rows_of(place + 1 - self.c)], axis=0)
        step = self.width // self.CHUNKS

        def chunk(i, carry):
            cols = pl.ds(pl.multiple_of(i * step, step), step)
            both = lax.dot_general(left, self.weight[cols, :], (((1,), (1,)), ((), ())), preferred_element_type=F32)
            self.box[k, :, cols] = both[self.rows:]
            self.mine[k, :, cols] = both[:self.rows]
            return carry

        lax.fori_loop(0, self.CHUNKS, chunk, 0)

    def pass_on(self, k):
        self.produce(k)
        self.copy(k).start()

    def pair_sum(self, k):
        self.wait_recv(k)

        def add(rows):
            self.mine[k, rows, :] = self.mine[k, rows, :] + self.pair[k, rows, :]

        row_loop(self.rows, add)

    def send_near(self):
        self.pass_on(0)
        self.pass_on(1)
        self.pair_sum(0)
        self.copy(4).start()
        self.copy(5).start()
        self.pass_on(2)
        self.pair_sum(1)
        self.copy(6).start()
        self.pass_on(3)
        self.pair_sum(2)
        self.copy(7).start()

    def send_far(self):
        self.wait_recv(4)

        def add_lo(rows):
            self.mine[1, rows, self.lo] = self.mine[1, rows, self.lo] + self.far[0, rows, :]

        row_loop(self.rows, add_lo)
        self.copy(8).start()
        self.wait_recv(5)

        def add_hi(rows):
            self.mine[2, rows, self.hi] = self.mine[2, rows, self.hi] + self.far[1, rows, :]

        row_loop(self.rows, add_hi)
        self.copy(9).start()

    def arrive(self):
        self.pair_sum(3)
        for i in (6, 8, 7, 9):
            self.wait_recv(i)

    def total(self, rows):
        return self.mine[3, rows, :] + self.near[0, rows, :] + self.near[1, rows, :]

    def finish(self):
        for i in range(self.SEMS):
            self.copy(i).wait_send()

    SCRATCH = 7

    @classmethod
    def scratch(cls, units, pos, width):
        return [pltpu.VMEM((units, 4, pos, width), F32), pltpu.VMEM((units, 4, pos, width), F32),
                pltpu.VMEM((units, 4, pos, width), F32),
                pltpu.VMEM((units, 2, pos, width // 2), F32), pltpu.VMEM((units, 2, pos, width), F32),
                pltpu.SemaphoreType.DMA((units, cls.SEMS)), pltpu.SemaphoreType.DMA((units, cls.SEMS))]

    @classmethod
    def of(cls, u, rows_of, weight, scratch):
        return cls(rows_of, weight, *(ref.at[u] for ref in scratch))


def gather_scratch(units):
    return [pltpu.SemaphoreType.DMA((units, Gather.SEMS)), pltpu.SemaphoreType.DMA((units, Gather.SEMS)),
            pltpu.SemaphoreType.DMA((units,))]


def gather_of(u, src, out, sems):
    send, recv, local = sems
    return Gather(src, out, send.at[u], recv.at[u], local.at[u])


def norm_rows(x_f32, gain):
    inv_rms = lax.rsqrt(jnp.mean(x_f32 * x_f32, axis=-1, keepdims=True) + NORM_EPS)
    return x_f32 * inv_rms * gain


def norm_rows_back(x_f32, gain, cotangent):
    inv_rms = lax.rsqrt(jnp.mean(x_f32 * x_f32, axis=-1, keepdims=True) + NORM_EPS)
    x_hat = x_f32 * inv_rms
    scaled = cotangent * gain
    inner = jnp.mean(scaled * x_hat, axis=-1, keepdims=True)
    return inv_rms * (scaled - x_hat * inner), cotangent * x_hat


def enter_kernel(x_ref, dy_ref, gain_ref, wqkv_ref, wout_ref, h_out, dy_out, w_out, h_src, w_src, *sems):
    n_seq, pos = x_ref.shape[:2]
    g_sems, w_sems = sems[:3], sems[3:]
    qkv_cols = wqkv_ref.shape[1]
    w_src[:, :qkv_cols] = wqkv_ref[...]
    w_src[:, qkv_cols:] = wout_ref[...]
    for s in range(n_seq):
        def norm(rows):
            h_src[s, rows, :] = norm_rows(x_ref[s, rows, :].astype(F32), gain_ref[...]).astype(BF16)

        row_loop(pos, norm)
    weights = WeightGather(w_src, w_out, *w_sems)
    _, _, other, nxt, prv = model_peers()
    sem = pltpu.get_barrier_semaphore()
    for peer in weights.barrier_peers():
        pl.semaphore_signal(sem, inc=1, device_id={'fsdp': peer}, device_id_type=MESH)
    for peer in (other, nxt, prv):
        pl.semaphore_signal(sem, inc=1, device_id={'model': peer}, device_id_type=MESH)
    pl.semaphore_wait(sem, 7)
    units = [gather_of(s, h_src.at[s], h_out.at[s], g_sems) for s in range(n_seq)]
    units += [gather_of(n_seq + s, dy_ref.at[s], dy_out.at[s], g_sems) for s in range(n_seq)]
    weights.begin()
    for unit in units:
        unit.begin()
    weights.step_near()
    units[0].forward_near()
    weights.step_own()
    weights.step_far()
    units[1].forward_near()
    weights.step_second(3)
    weights.step_second(1)
    units[2].forward_near()
    weights.step_second(2)
    units[3].forward_near()
    for unit in units:
        unit.forward_far()
    weights.finish()
    for unit in units:
        unit.finish()


def load_rows(refs, s, pos):
    def rows_of(place):
        rows = pl.ds(pl.multiple_of(place * pos, pos), pos)
        return jnp.concatenate([ref[s, rows, :] for ref in refs], axis=1)

    return rows_of


def fetch_weight(w_hbm, first_col, w_vmem, sem):
    return pltpu.make_async_copy(w_hbm.at[:, pl.ds(first_col, w_vmem.shape[1])], w_vmem, sem)


def middle_kernel(backward, first_col, n_left, *refs):
    left, refs = refs[:n_left], refs[n_left:]
    w_hbm, base_ref, mid_ref, gain_ref, res_ref, full_out, dgain_ref = refs[:7]
    scratch = refs[7:]
    n_seq, pos = base_ref.shape[:2]
    rs_scratch, scratch = scratch[:Scatter.SCRATCH], scratch[Scatter.SCRATCH:]
    w_vmem, w_sem, g_src, sums = scratch[:4]
    sems = scratch[4:]
    fetch_weight(w_hbm, first_col, w_vmem, w_sem).start()
    _, _, other, nxt, prv = model_peers()
    model_barrier((other, nxt, prv))
    units = [Scatter.of(s, load_rows(left, s, pos), w_vmem, rs_scratch) for s in range(n_seq)]
    sends = [gather_of(s, g_src.at[s], full_out.at[s], sems) for s in range(n_seq)]
    if backward:
        sums[...] = jnp.zeros_like(sums)

    def settle(s):
        units[s].arrive()

        def rows_fn(rows):
            red = units[s].total(rows).astype(BF16).astype(F32)
            if backward:
                d_norm, d_gain = norm_rows_back(mid_ref[s, rows, :].astype(F32), gain_ref[...], red)
                out = (base_ref[s, rows, :].astype(F32) + d_norm).astype(BF16)
                sums[...] += d_gain
                res_ref[s, rows, :] = out
                g_src[s, rows, :] = out
            else:
                mid = (base_ref[s, rows, :].astype(F32) + red).astype(BF16)
                res_ref[s, rows, :] = mid
                g_src[s, rows, :] = norm_rows(mid.astype(F32), gain_ref[...]).astype(BF16)

        row_loop(pos, rows_fn)

    fetch_weight(w_hbm, first_col, w_vmem, w_sem).wait()
    units[0].send_near()
    units[0].send_far()
    for s in range(n_seq):
        if s + 1 < n_seq:
            units[s + 1].send_near()
        settle(s)
        sends[s].begin()
        if s + 1 < n_seq:
            units[s + 1].send_far()
    for unit in sends:
        unit.forward_near()
    for unit in sends:
        unit.forward_far()
    if backward:
        dgain_ref[...] = jnp.sum(sums[...], axis=0, keepdims=True)
    else:
        dgain_ref[...] = jnp.zeros_like(dgain_ref)
    for unit in units:
        unit.finish()
    for unit in sends:
        unit.finish()


def leave_kernel(backward, first_col, left_ref, w_hbm, base_ref, x_ref, gain_ref, res_ref, dgain_ref, *scratch):
    n_seq, pos = base_ref.shape[:2]
    rs_scratch, (w_vmem, w_sem, sums) = scratch[:Scatter.SCRATCH], scratch[Scatter.SCRATCH:]
    fetch_weight(w_hbm, first_col, w_vmem, w_sem).start()
    _, _, other, nxt, prv = model_peers()
    model_barrier((other, nxt, prv))
    sums[...] = jnp.zeros_like(sums)
    units = [Scatter.of(s, load_rows([left_ref], s, pos), w_vmem, rs_scratch) for s in range(n_seq)]

    def settle(s):
        units[s].arrive()

        def rows_fn(rows):
            red = units[s].total(rows).astype(BF16).astype(F32)
            if backward:
                red, d_gain = norm_rows_back(x_ref[s, rows, :].astype(F32), gain_ref[...], red)
                sums[...] += d_gain
            res_ref[s, rows, :] = (base_ref[s, rows, :].astype(F32) + red).astype(BF16)

        row_loop(pos, rows_fn)

    fetch_weight(w_hbm, first_col, w_vmem, w_sem).wait()
    units[0].send_near()
    units[0].send_far()
    for s in range(n_seq):
        if s + 1 < n_seq:
            units[s + 1].send_near()
            units[s + 1].send_far()
        settle(s)
    dgain_ref[...] = jnp.sum(sums[...], axis=0, keepdims=True)
    for unit in units:
        unit.finish()


def spin(tensor, cos_t, sin_t):
    return tensor * cos_t + pltpu.roll(tensor, tensor.shape[1] // 2, 1) * sin_t


def probs(query, key, scale, first_row):
    scores = lax.dot_general(query, key, (((1,), (1,)), ((), ())), preferred_element_type=F32) * scale
    rows = first_row + lax.broadcasted_iota(jnp.int32, scores.shape, 0)
    cols = lax.broadcasted_iota(jnp.int32, scores.shape, 1)
    scores = jnp.where(rows >= cols, scores, -1e30)
    expd = jnp.exp(scores - jnp.max(scores, axis=-1, keepdims=True))
    return expd / jnp.sum(expd, axis=-1, keepdims=True)


def attn_kernel(heads, group, scale, h_ref, w_ref, cos_ref, sin_ref, qkv_ref, attn_ref):
    seq, head_dim = cos_ref.shape
    block = seq // 2
    n_groups = heads // group
    cols = qkv_ref.shape[2]

    def lanes(i):
        return slice(i * head_dim, (i + 1) * head_dim)

    def project(i, carry):
        rows = pl.ds(pl.multiple_of(i * block, block), block)
        qkv = jnp.dot(h_ref[0, rows, :], w_ref[:, :cols], preferred_element_type=F32)
        cos_t, sin_t = cos_ref[rows, :], sin_ref[rows, :]
        for j in range(cols // head_dim):
            one = qkv[:, lanes(j)]
            if j % (group + 2) <= group:
                one = spin(one, cos_t, sin_t)
            qkv_ref[0, rows, lanes(j)] = one.astype(BF16)
        return carry

    lax.fori_loop(0, seq // block, project, 0)
    for g in range(n_groups):
        first = g * (group + 2)
        for i in range(seq // block):
            rows, keys = slice(i * block, (i + 1) * block), slice(0, (i + 1) * block)
            key, value = qkv_ref[0, keys, lanes(first + group)], qkv_ref[0, keys, lanes(first + group + 1)]
            for j in range(group):
                prob = probs(qkv_ref[0, rows, lanes(first + j)], key, scale, i * block)
                attn_ref[0, rows, lanes(g * group + j)] = jnp.dot(
                    prob.astype(BF16), value, preferred_element_type=F32).astype(BF16)


def attn_back_kernel(heads, group, scale, dm_ref, w_ref, cos_ref, sin_ref, qkv_ref, dqkv_ref, do_ref, dk_ref, dv_ref):
    seq, head_dim = cos_ref.shape
    block = seq // 2
    n_groups = heads // group
    cols = qkv_ref.shape[2]

    def lanes(i):
        return slice(i * head_dim, (i + 1) * head_dim)

    def project(i, carry):
        rows = pl.ds(pl.multiple_of(i * block, block), block)
        do_ref[rows, :] = jnp.dot(dm_ref[0, rows, :], w_ref[:, cols:], preferred_element_type=F32).astype(BF16)
        return carry

    lax.fori_loop(0, seq // block, project, 0)
    over_rows = (((0,), (0,)), ((), ()))
    for g in range(n_groups):
        first = g * (group + 2)
        dk_ref[...] = jnp.zeros_like(dk_ref)
        dv_ref[...] = jnp.zeros_like(dv_ref)
        for i in range(seq // block):
            rows, keys = slice(i * block, (i + 1) * block), slice(0, (i + 1) * block)
            key, value = qkv_ref[0, keys, lanes(first + group)], qkv_ref[0, keys, lanes(first + group + 1)]
            for j in range(group):
                query = qkv_ref[0, rows, lanes(first + j)]
                d_out = do_ref[rows, lanes(g * group + j)]
                prob = probs(query, key, scale, i * block)
                d_prob = lax.dot_general(d_out, value, (((1,), (1,)), ((), ())), preferred_element_type=F32)
                row_dot = jnp.sum(d_prob * prob, axis=-1, keepdims=True)
                d_scores = (prob * (d_prob - row_dot) * scale).astype(BF16)
                d_query = jnp.dot(d_scores, key, preferred_element_type=F32)
                dqkv_ref[0, rows, lanes(first + j)] = spin(d_query, cos_ref[rows, :], -sin_ref[rows, :]).astype(BF16)
                dk_ref[keys, :] += lax.dot_general(d_scores, query, over_rows, preferred_element_type=F32)
                dv_ref[keys, :] += lax.dot_general(prob.astype(BF16), d_out, over_rows, preferred_element_type=F32)
        dqkv_ref[0, :, lanes(first + group)] = spin(dk_ref[...], cos_ref[...], -sin_ref[...]).astype(BF16)
        dqkv_ref[0, :, lanes(first + group + 1)] = dv_ref[...].astype(BF16)


def mlp_kernel(h_ref, dy_ref, wg_ref, wu_ref, wd_ref, act_ref, dgu_ref):
    tokens = h_ref.shape[0]
    block = tokens // 4

    def rows_fn(i, carry):
        rows = pl.ds(pl.multiple_of(i * block, block), block)
        gate = jnp.dot(h_ref[rows, :], wg_ref[...], preferred_element_type=F32)
        up_proj = jnp.dot(h_ref[rows, :], wu_ref[...], preferred_element_type=F32)
        d_act = jnp.dot(dy_ref[rows, :], wd_ref[...], preferred_element_type=F32).astype(BF16).astype(F32)
        sig_gate = jax.nn.sigmoid(gate)
        silu_gate = gate * sig_gate
        act_ref[rows, :] = (silu_gate * up_proj).astype(BF16)
        dgu_ref[0, rows, :] = (d_act * up_proj * sig_gate * (1.0 + gate * (1.0 - sig_gate))).astype(BF16)
        dgu_ref[1, rows, :] = (d_act * silu_gate).astype(BF16)
        return carry

    lax.fori_loop(0, tokens // block, rows_fn, 0)


def grad_kernel(n_first, *refs):
    one_ref, two_ref = refs[:2]
    first, second, out_ref = refs[2], refs[3], refs[4]
    over_rows = (((0,), (0,)), ((), ()))
    col = 0
    for i in range(n_first):
        right = first[i]
        out_ref[:, col:col + right.shape[1]] = lax.dot_general(one_ref[...], right, over_rows, preferred_element_type=F32)
        col += right.shape[1]
    out_ref[:, col:] = lax.dot_general(two_ref[...], second[...], over_rows, preferred_element_type=F32)


def gain_kernel(part_ref, out_ref, total, slots, send, recv):
    m = lax.axis_index('model')
    f = lax.axis_index('fsdp')
    x, c = m // 2, m % 2
    z, y = f // 4, f % 4
    stages = [[(f, 2 * x + (1 - c))],
              [(f, 2 * ((x + d) % 4) + c) for d in (1, 2, 3)],
              [(4 * z + (y + d) % 4, m) for d in (1, 2, 3)],
              [(4 * ((z + d) % 4) + y, m) for d in (1, 2, 3)]]
    places = [c, x, y, z]
    sem = pltpu.get_barrier_semaphore()
    n_peers = 0
    for peers in stages:
        for ff, mm in peers:
            pl.semaphore_signal(sem, inc=1, device_id={'fsdp': ff, 'model': mm}, device_id_type=MESH)
            n_peers += 1
    total[0] = part_ref[...]
    pl.semaphore_wait(sem, n_peers)
    for t, peers in enumerate(stages):
        n = len(peers) + 1
        place = places[t]
        copies = []
        for d, (ff, mm) in enumerate(peers):
            copies.append(pltpu.make_async_remote_copy(
                src_ref=total.at[t], dst_ref=slots.at[t, d], send_sem=send.at[t, d], recv_sem=recv.at[t, d],
                device_id={'fsdp': ff, 'model': mm}, device_id_type=MESH))
            copies[-1].start()
        for copy in copies:
            copy.wait_recv()
        terms = [total[t]] + [slots[t, d] for d in range(n - 1)]
        acc = None
        for place_i in range(n):
            term = terms[0]
            for d in range(n - 1):
                term = jnp.where((place + n - (d + 1)) % n == place_i, terms[d + 1], term)
            acc = term if acc is None else acc + term
        total[t + 1] = acc
        for copy in copies:
            copy.wait_send()
    out_ref[...] = total[len(stages)]


def solution(mesh):
    act_spec = P('fsdp', 'model', None)
    rows_spec = P('fsdp', 'model')
    cols_spec = P('model', 'fsdp')

    def device_fn(x_loc, dy_loc, gain_attn, gain_mlp, wqkv_sh, wout_sh, wgate_sh, wup_sh, wdown_sh, rope_cos, rope_sin):
        n_seq, pos, width = x_loc.shape
        seq = rope_cos.shape[0]
        tokens = n_seq * seq
        n_model = seq // pos
        head_dim = 2 * rope_cos.shape[1]
        heads = wout_sh.shape[0] // head_dim
        shard_rows, qkv_cols = wqkv_sh.shape
        out_rows, ff = wout_sh.shape[0], wgate_sh.shape[1]
        n_fsdp = width // shard_rows
        attn_cols = qkv_cols + out_rows
        kv = (qkv_cols // head_dim - heads) // 2
        group = heads // kv
        scale = head_dim ** -0.5
        gain_a, gain_m = gain_attn[None, :], gain_mlp[None, :]
        cos_t = jnp.concatenate([rope_cos, rope_cos], axis=1)
        sin_t = jnp.concatenate([-rope_sin, rope_sin], axis=1)

        vmem = pl.BlockSpec(memory_space=pltpu.VMEM)
        hbm = pl.BlockSpec(memory_space=pl.ANY)
        local_bf = jax.ShapeDtypeStruct((n_seq, pos, width), BF16)
        full_bf = jax.ShapeDtypeStruct((n_seq, n_model, pos, width), BF16)
        row_f32 = jax.ShapeDtypeStruct((1, width), F32)

        def params(cid):
            return pltpu.CompilerParams(collective_id=cid, has_side_effects=True, vmem_limit_bytes=60 * 2 ** 20)

        plain = pltpu.CompilerParams(vmem_limit_bytes=60 * 2 ** 20)

        def cost(flops, nbytes):
            return pl.CostEstimate(flops=int(flops), bytes_accessed=int(nbytes), transcendentals=0)

        def scatter_w(grad):
            return lax.psum_scatter(grad, 'fsdp', scatter_dimension=0, tiled=True)

        w_mlp = lax.all_gather(jnp.concatenate([wgate_sh, wup_sh, wdown_sh.T], axis=1), 'fsdp', axis=0, tiled=True)

        h_full, dy_full, w_attn = pl.pallas_call(
            enter_kernel,
            out_shape=(full_bf, full_bf, jax.ShapeDtypeStruct((n_fsdp, shard_rows, attn_cols), BF16)),
            in_specs=[vmem] * 5, out_specs=(hbm,) * 3,
            scratch_shapes=[pltpu.VMEM((n_seq, pos, width), BF16), pltpu.VMEM((shard_rows, attn_cols), BF16)]
            + gather_scratch(2 * n_seq)
            + [pltpu.SemaphoreType.DMA((WeightGather.SEMS, RingGather.SEMS)),
               pltpu.SemaphoreType.DMA((WeightGather.SEMS, RingGather.SEMS)), pltpu.SemaphoreType.DMA],
            compiler_params=params(0), name='enter', cost_estimate=cost(6e10, 2e7),
        )(x_loc, dy_loc, gain_a, wqkv_sh, wout_sh.T)
        h_attn = h_full.reshape(tokens, width)
        dy_full = dy_full.reshape(tokens, width)
        w_attn = w_attn.reshape(width, attn_cols)

        def per_seq(cols):
            return pl.BlockSpec((1, seq, cols), lambda s: (s, 0, 0))

        def whole(shape):
            return pl.BlockSpec(shape, lambda *_: (0,) * len(shape))

        qkv, attn = pl.pallas_call(
            functools.partial(attn_kernel, heads, group, scale), grid=(n_seq,),
            out_shape=(jax.ShapeDtypeStruct((n_seq, seq, qkv_cols), BF16),
                       jax.ShapeDtypeStruct((n_seq, seq, out_rows), BF16)),
            in_specs=[per_seq(width), whole((width, attn_cols)), whole((seq, head_dim)), whole((seq, head_dim))],
            out_specs=(per_seq(qkv_cols), per_seq(out_rows)), compiler_params=plain, name='attn',
            cost_estimate=cost(5e9, 2e7),
        )(h_attn.reshape(n_seq, seq, width), w_attn, cos_t, sin_t)

        def middle(backward, cid, left, w, first_col, base, mid):
            depth = sum(a.shape[-1] for a in left)
            scratch = (Scatter.scratch(n_seq, pos, width)
                       + [pltpu.VMEM((width, depth), BF16), pltpu.SemaphoreType.DMA,
                          pltpu.VMEM((n_seq, pos, width), BF16), pltpu.VMEM((ROWS, width), F32)]
                       + gather_scratch(n_seq))
            return pl.pallas_call(
                functools.partial(middle_kernel, backward, first_col, len(left)), out_shape=(local_bf, full_bf, row_f32),
                in_specs=[vmem] * len(left) + [hbm] + [vmem] * 3, out_specs=(vmem, hbm, vmem), scratch_shapes=scratch,
                compiler_params=params(cid), name='middle_bwd' if backward else 'middle_fwd',
                cost_estimate=cost(9e10, 2e7),
            )(*left, w, base, mid, gain_m)

        mid, h_mlp, _ = middle(False, 1, [attn], w_attn, qkv_cols, x_loc, x_loc)
        h_mlp = h_mlp.reshape(tokens, width)

        n_cols = 4
        ff_block = ff // n_cols

        def w_cols(part):
            return pl.BlockSpec((width, ff_block), lambda j: (0, part * n_cols + j))

        act, d_gu = pl.pallas_call(
            mlp_kernel, grid=(n_cols,),
            out_shape=(jax.ShapeDtypeStruct((tokens, ff), BF16), jax.ShapeDtypeStruct((2, tokens, ff), BF16)),
            in_specs=[whole((tokens, width)), whole((tokens, width)), w_cols(0), w_cols(1), w_cols(2)],
            out_specs=(pl.BlockSpec((tokens, ff_block), lambda j: (0, j)),
                       pl.BlockSpec((2, tokens, ff_block), lambda j: (0, 0, j))),
            compiler_params=plain, name='mlp', cost_estimate=cost(2e10, 4e7),
        )(h_mlp, dy_full, w_mlp, w_mlp, w_mlp)

        def weight_grads(one, two, first, second, block):
            n_first, _, cols = first.shape
            total = n_first * cols + second.shape[1]
            lhs = pl.BlockSpec((tokens, block), lambda i: (0, i))
            return pl.pallas_call(
                functools.partial(grad_kernel, n_first), grid=(width // block,),
                out_shape=jax.ShapeDtypeStruct((width, total), F32),
                in_specs=[lhs, lhs, whole(first.shape), whole(second.shape)],
                out_specs=pl.BlockSpec((block, total), lambda i: (i, 0)), compiler_params=plain,
                cost_estimate=cost(2 * tokens * width * total, 4 * width * total),
            )(one, two, first, second)

        dw_mlp = weight_grads(h_mlp, dy_full, d_gu, act, width // 12)
        rs_mlp = scatter_w(dw_mlp)
        d_gate, d_up, dw_mlp = lax.optimization_barrier((d_gu[0], d_gu[1], dw_mlp))

        def by_seq(arr):
            return arr.reshape(n_seq, seq, arr.shape[-1])

        d_mid, d_mid_full, dgain_mlp = middle(True, 2, [by_seq(d_gate), by_seq(d_up)], w_mlp, 0, dy_loc, mid)
        d_mid_full = d_mid_full.reshape(tokens, width)

        d_qkv = pl.pallas_call(
            functools.partial(attn_back_kernel, heads, group, scale), grid=(n_seq,),
            out_shape=jax.ShapeDtypeStruct((n_seq, seq, qkv_cols), BF16),
            in_specs=[per_seq(width), whole((width, attn_cols)), whole((seq, head_dim)), whole((seq, head_dim)),
                      per_seq(qkv_cols)],
            out_specs=per_seq(qkv_cols),
            scratch_shapes=[pltpu.VMEM((seq, out_rows), BF16), pltpu.VMEM((seq, head_dim), F32),
                            pltpu.VMEM((seq, head_dim), F32)],
            compiler_params=plain, name='attn_back', cost_estimate=cost(5e9, 2e7),
        )(d_mid_full.reshape(n_seq, seq, width), w_attn, cos_t, sin_t, qkv)

        dw_attn = weight_grads(h_attn, d_mid_full, d_qkv.reshape(1, tokens, qkv_cols), attn.reshape(tokens, out_rows),
                               width // 12)
        rs_attn = scatter_w(dw_attn)
        d_qkv, dw_attn = lax.optimization_barrier((d_qkv, dw_attn))

        def leave(backward, cid, left, w, first_col, base, x):
            return pl.pallas_call(
                functools.partial(leave_kernel, backward, first_col), out_shape=(local_bf, row_f32),
                in_specs=[vmem, hbm] + [vmem] * 3, out_specs=(vmem,) * 2,
                scratch_shapes=Scatter.scratch(n_seq, pos, width)
                + [pltpu.VMEM((width, left.shape[-1]), BF16), pltpu.SemaphoreType.DMA, pltpu.VMEM((ROWS, width), F32)],
                compiler_params=params(cid), name='leave_dx' if backward else 'leave_y', cost_estimate=cost(6e10, 2e7),
            )(left, w, base, x, gain_a)

        dx, dgain_attn = leave(True, 3, d_qkv, w_attn, 0, d_mid, x_loc)
        act, dgain_attn = lax.optimization_barrier((by_seq(act), dgain_attn))
        y, _ = leave(False, 5, act, w_mlp, 2 * ff, mid, x_loc)
        gain_part = jnp.concatenate([dgain_attn, dgain_mlp], axis=0).reshape(16, 2 * width // 16)
        gain_sum = pl.pallas_call(
            gain_kernel, out_shape=jax.ShapeDtypeStruct(gain_part.shape, F32), in_specs=[vmem], out_specs=vmem,
            scratch_shapes=[pltpu.VMEM((5,) + gain_part.shape, F32), pltpu.VMEM((4, 3) + gain_part.shape, F32),
                            pltpu.SemaphoreType.DMA((4, 3)), pltpu.SemaphoreType.DMA((4, 3))],
            compiler_params=params(4), name='gains', cost_estimate=cost(1e10, 1e5),
        )(gain_part).reshape(2, width)
        return (y, dx, gain_sum[0], gain_sum[1], rs_attn[:, :qkv_cols], rs_attn[:, qkv_cols:].T,
                rs_mlp[:, :ff], rs_mlp[:, ff:2 * ff], rs_mlp[:, 2 * ff:].T)

    in_specs = (act_spec, act_spec, P(), P(), rows_spec, cols_spec, rows_spec, rows_spec, cols_spec, P(), P())
    out_specs = (act_spec, act_spec, P(), P(), rows_spec, cols_spec, rows_spec, rows_spec, cols_spec)
    return jax.shard_map(device_fn, mesh=mesh, in_specs=in_specs, out_specs=out_specs, check_vma=False)
```

time: 1440 us -> 710 us (0.49)
  waiting for transfers between devices: 1090 us -> 160 us
  Pallas kernels: 0 us -> 514 us
  matrix products: 212 us -> 0 us
  blocking collectives: 68.5 us -> 0 us
  other arithmetic: 29.2 us -> 4.14 us
    pallas_call x0 -> x11, Pallas kernels: none -> 514 us  [the longest x2 195 us: middle(): pl.pallas_call(functools.partial(middle_kernel, backward, first_col, len(...]
    reduce_scatter x13 -> x2, waiting for transfers between devices: 628 us -> 160 us  [scatter_w(): return lax.psum_scatter(grad, 'fsdp', scatter_dimension=0, tiled=True)]
    all_gather x13 -> x1, waiting for transfers between devices: 454 us -> 0.02 us  [device_fn(): lax.all_gather(jnp.concatenate([wgate_sh, wup_sh, wdown_sh.T], axis=1), '...]
    dot_general x42 -> x0, matrix products: 212 us -> none  [the longest x2 22.3 us: micro_step(): jnp.einsum('bsf,df->bsd', d_up, w_up_b, preferred_element_type=jnp.float32)]
    psum x1 -> x0, blocking collectives: 68.5 us -> none  [device_fn(): gain_grads = lax.psum((accum[0], accum[1]), ('fsdp', 'model'))]
  transfers between devices with their start and end apart: 26 -> 3, of which waited for: 25 -> 1; matrix products, arithmetic and copies ran while one was open for 12% -> 1% of each run, Pallas kernels for 0% -> 45%
where the time goes in v1:
time: 710 us; the launch traced here: 708 us
  Pallas kernels  514 us (72%)
  waiting for transfers between devices  160 us (23%)
  local copies, waits for them, and re-layouts  16 us (2%)
  between operations  13.9 us (2%)
    pallas_call x2, Pallas kernels, middle(): pl.pallas_call(functools.partial(middle_kernel, backward, first_col, len(...  195 us
    reduce_scatter x2, waiting for transfers between devices, scatter_w(): return lax.psum_scatter(grad, 'fsdp', scatter_dimension=0, tiled=True)  160 us
    pallas_call x2, Pallas kernels, leave(): pl.pallas_call(functools.partial(leave_kernel, backward, first_col), out_...  128 us
    pallas_call x1, Pallas kernels, device_fn(): pl.pallas_call(enter_kernel, out_shape=(full_bf, full_bf, jax.ShapeDtypeS...  66.7 us
    pallas_call x2, Pallas kernels, weight_grads(): pl.pallas_call(functools.partial(grad_kernel, n_first), grid=(width // bl...  45.7 us
    pallas_call x1, Pallas kernels, device_fn(): pl.pallas_call(mlp_kernel, grid=(n_cols,), out_shape=(jax.ShapeDtypeStruc...  30.5 us
    pallas_call x1, Pallas kernels, device_fn(): pl.pallas_call(functools.partial(attn_back_kernel, heads, group, scale),...  16.8 us
    pallas_call x1, Pallas kernels, device_fn(): pl.pallas_call(gain_kernel, out_shape=jax.ShapeDtypeStruct(gain_part.shap...  16.3 us
  transfers between devices with their start and end apart: 3, of which 1 were waited for; matrix products, arithmetic and copies ran while one was open for 1% of the time, Pallas kernels for 45%

profile of v1, /device:TPU:1, one launch (start us, length us, event | category | flops | bytes accessed | tf_op | source)
XLA Modules:
  0.0 708.5 jit_solution(6266829699394160941)
XLA Ops:
  7.2 0.0 all-gather.2.cloned.1.call-start
  7.2 2.4 pad_maximum_fusion
  9.7 0.0 reduce-scatter.3.cloned.1.call-start
  9.7 0.1 copy.27
  9.9 0.1 copy.26
  10.0 0.1 copy.24
  10.1 1.0 pad_maximum_fusion.1
  11.1 66.7 %enter.1 = (bf16[2,8,64,3072]{3,2,1,0:T(8,128)(2,1)}, bf16[2,8,64,3072]{3,2,1,0:T(8,128)(2,1)}, bf16[16,192,1024]{2,1,0:T(8,128)(2,1)}) custom-call(bf16[2,64,3072]{2,1,0:T(8,128)(2,1)} %x_ref.5, bf16[2,64,3072]{2,1,0:T(8,128)(2,1)} %refs_3_.3, f32[1,3072]{1,0:T(1,128)} %bitcast.36, bf16[192,640]{1,0:T(8,128)(2,1)} %wqkv_ref.1, bf16[192,384]{1,0:T(8,128)(2,1)} %bitcast.33), custom_call_target="tpu_custom_call" | custom-call | flops 60000002048 | bytes 20000000 | tf_op jit(solution)/shard_map/enter/pallas_call | solution.py:705
  77.9 15.0 %attn.1 = (bf16[2,512,640]{2,1,0:T(8,128)(2,1)}, bf16[2,512,384]{2,1,0:T(8,128)(2,1)}) custom-call(bf16[2,512,3072]{2,1,0:T(8,128)(2,1)} %bitcast.24, bf16[3072,1024]{1,0:T(8,128)(2,1)} %bitcast.39, f32[512,128]{1,0:T(8,128)} %get-tuple-element.56.cos_ref, f32[512,128]{1,0:T(8,128)} %get-tuple-element.57.sin_ref), custom_call_target="tpu_custom_call" | custom-call | flops 5000000000 | bytes 20000000 | tf_op jit(solution)/shard_map/attn/pallas_call | solution.py:725
  92.9 91.6 %middle_fwd.1 = (bf16[2,64,3072]{2,1,0:T(8,128)(2,1)}, bf16[2,8,64,3072]{3,2,1,0:T(8,128)(2,1)}, f32[1,3072]{1,0:T(1,128)}) custom-call(bf16[2,512,384]{2,1,0:T(8,128)(2,1)} %get-tuple-element.31.refs_0_, bf16[3072,1024]{1,0:T(8,128)(2,1)} %bitcast.40, bf16[2,64,3072]{2,1,0:T(8,128)(2,1)} %x_ref.5, bf16[2,64,3072]{2,1,0:T(8,128)(2,1)} %x_ref.5, ...), custom_call_target="tpu_custom_call" | custom-call | flops 89999998976 | bytes 20000000 | tf_op jit(solution)/shard_map/middle_fwd/pallas_call | solution.py:740
  184.5 30.5 %mlp.1 = (bf16[1024,1024]{1,0:T(8,128)(2,1)}, bf16[2,1024,1024]{2,1,0:T(8,128)(2,1)}) custom-call(bf16[1024,3072]{1,0:T(8,128)(2,1)} %bitcast.45, bf16[1024,3072]{1,0:T(8,128)(2,1)} %bitcast.43, bf16[3072,3072]{1,0:T(8,128)(2,1)} %all-gather.2.cloned.1.call-done.wg_ref.wu_ref.wd_ref.refs_2_.w_hbm, ...), custom_call_target="tpu_custom_call" | custom-call | flops 20000000000 | bytes 40000000 | tf_op jit(solution)/shard_map/mlp/pallas_call | solution.py:756
  215.0 4.7 slice_bitcast_fusion
  219.7 28.1 %shard_map.178 = f32[3072,3072]{1,0:T(8,128)} custom-call(bf16[1024,3072]{1,0:T(8,128)(2,1)} %bitcast.46, bf16[1024,3072]{1,0:T(8,128)(2,1)} %bitcast.44, bf16[2,1024,1024]{2,1,0:T(8,128)(2,1)} %get-tuple-element.35.refs_2_, bf16[1024,1024]{1,0:T(8,128)(2,1)} %get-tuple-element.34.refs_3_), custom_call_target="tpu_custom_call" | custom-call | flops 19327352832 | bytes 37748736 | tf_op jit(solution)/shard_map/pallas_call | solution.py:769
  247.9 103.2 %middle_bwd.1 = (bf16[2,64,3072]{2,1,0:T(8,128)(2,1)}, bf16[2,8,64,3072]{3,2,1,0:T(8,128)(2,1)}, f32[1,3072]{1,0:T(1,128)}) custom-call(bf16[2,512,1024]{2,1,0:T(8,128)(2,1)} %bitcast.29, bf16[2,512,1024]{2,1,0:T(8,128)(2,1)} %bitcast.28, bf16[3072,3072]{1,0:T(8,128)(2,1)} %all-gather.2.cloned.1.call-done.wg_ref.wu_ref.wd_ref.refs_2_.w_hbm, ...), custom_call_target="tpu_custom_call" | custom-call | flops 89999998976 | bytes 20000000 | tf_op jit(solution)/shard_map/middle_bwd/pallas_call | solution.py:740
  351.1 16.8 %attn_back.1.left_ref = bf16[2,512,640]{2,1,0:T(8,128)(2,1)} custom-call(bf16[2,512,3072]{2,1,0:T(8,128)(2,1)} %bitcast.26, bf16[3072,1024]{1,0:T(8,128)(2,1)} %bitcast.41, f32[512,128]{1,0:T(8,128)} %get-tuple-element.56.cos_ref, f32[512,128]{1,0:T(8,128)} %get-tuple-element.57.sin_ref, bf16[2,512,640]{2,1,0:T(8,128)(2,1)} %get-tuple-element.40.qkv_ref), custom_call_target="tpu_custom_call" | custom-call | flops 5000000000 | bytes 20000000 | tf_op jit(solution)/shard_map/attn_back/pallas_call | solution.py:787
  367.9 17.5 %shard_map.179 = f32[3072,1024]{1,0:T(8,128)} custom-call(bf16[1024,3072]{1,0:T(8,128)(2,1)} %bitcast.25, bf16[1024,3072]{1,0:T(8,128)(2,1)} %bitcast.27, bf16[1,1024,640]{2,1,0:T(8,128)(2,1)} %bitcast.30, bf16[1024,384]{1,0:T(8,128)(2,1)} %bitcast.31), custom_call_target="tpu_custom_call" | custom-call | flops 6442450944 | bytes 12582912 | tf_op jit(solution)/shard_map/pallas_call | solution.py:769
  385.4 0.0 reduce-scatter.5.cloned.1.call-start
  385.5 0.7 reduce-scatter.5.cloned.1.call-update
  386.2 62.7 %leave_dx.1 = (bf16[2,64,3072]{2,1,0:T(8,128)(2,1)}, f32[1,3072]{1,0:T(1,128)}) custom-call(bf16[2,512,640]{2,1,0:T(8,128)(2,1)} %attn_back.1.left_ref, bf16[3072,1024]{1,0:T(8,128)(2,1)} %bitcast.42, bf16[2,64,3072]{2,1,0:T(8,128)(2,1)} %get-tuple-element.42.base_ref, bf16[2,64,3072]{2,1,0:T(8,128)(2,1)} %x_ref.5, f32[1,3072]{1,0:T(1,128)} %bitcast.37), custom_call_target="tpu_custom_call" | custom-call | flops 60000002048 | bytes 20000000 | tf_op jit(solution)/shard_map/leave_dx/pallas_call | solution.py:804
  448.9 0.7 pad_maximum_fusion.3
  449.6 0.6 reshape.66.part_ref
  450.2 16.3 %gains.1 = f32[16,384]{1,0:T(8,128)} custom-call(f32[16,384]{1,0:T(8,128)} %reshape.66.part_ref), custom_call_target="tpu_custom_call" | custom-call | flops 10000000000 | bytes 100000 | tf_op jit(solution)/shard_map/gains/pallas_call | solution.py:816
  466.5 0.7 fusion
  467.2 0.6 squeeze.14
  467.8 0.6 squeeze.15
  468.4 65.4 %leave_y.1 = (bf16[2,64,3072]{2,1,0:T(8,128)(2,1)}, f32[1,3072]{1,0:T(1,128)}) custom-call(bf16[2,512,1024]{2,1,0:T(8,128)(2,1)} %bitcast.47, bf16[3072,3072]{1,0:T(8,128)(2,1)} %all-gather.2.cloned.1.call-done.wg_ref.wu_ref.wd_ref.refs_2_.w_hbm, bf16[2,64,3072]{2,1,0:T(8,128)(2,1)} %get-tuple-element.38.refs_4_.base_ref, bf16[2,64,3072]{2,1,0:T(8,128)(2,1)} %x_ref.5, ...), custom_call_target="tpu_custom_call" | custom-call | flops 60000002048 | bytes 20000000 | tf_op jit(solution)/shard_map/leave_y/pallas_call | solution.py:804
  533.9 1.8 slice.38
  535.7 1.7 slice_bitcast_fusion.3
  537.4 159.6 %reduce-scatter.5.cloned.1.call-done = f32[192,3072]{1,0:T(8,128)} async-done(((f32[3072,3072]{1,0:T(8,128)}), f32[192,3072]{1,0:T(8,128)}) %reduce-scatter.5.cloned.1.call-update) | async-done | bytes 2359312 | tf_op jit(solution)/shard_map/reduce_scatter | solution.py:701
  697.1 3.1 slice_bitcast_fusion.2
  700.2 0.9 copy.30
  701.0 0.9 copy.31
  (15 shorter events, 0.1 us)
Async XLA Ops:
  7.2 2.5 copy-start.2
  7.2 2.8 copy-start.3
  7.2 177.3 %all-gather.2.cloned.1.call-start = ((), (), s32[]{:S(2)}) async-start(), calls=%async_computation.2 | async-start | bytes 20054016 | tf_op jit(solution)/shard_map/all_gather | solution.py:703
  9.7 524.2 %reduce-scatter.3.cloned.1.call-start = ((), (), s32[]{:S(2)}) async-start(), calls=%async_computation.3 | async-start | bytes 13369344 | tf_op jit(solution)/shard_map/reduce_scatter | solution.py:701
  385.4 311.7 %reduce-scatter.5.cloned.1.call-start = ((), (), s32[]{:S(2)}) async-start(), calls=%async_computation.4 | async-start | bytes 40108032 | tf_op jit(solution)/shard_map/reduce_scatter | solution.py:701
  386.1 62.7 %copy-start.4 = (f32[1,3072]{1,0:T(1,128)S(1)}, f32[1,3072]{1,0:T(1,128)}, u32[]{:S(2)}) copy-start(f32[1,3072]{1,0:T(1,128)} %get-tuple-element.48) | copy-start | bytes 36868
  537.4 162.7 %copy-start.1 = (bf16[2,64,3072]{2,1,0:T(8,128)(2,1)S(1)}, bf16[2,64,3072]{2,1,0:T(8,128)(2,1)}, u32[]{:S(2)}) copy-start(bf16[2,64,3072]{2,1,0:T(8,128)(2,1)} %get-tuple-element.67) | copy-start | bytes 2359300
  537.4 163.6 %copy-start = (bf16[2,64,3072]{2,1,0:T(8,128)(2,1)S(1)}, bf16[2,64,3072]{2,1,0:T(8,128)(2,1)}, u32[]{:S(2)}) copy-start(bf16[2,64,3072]{2,1,0:T(8,128)(2,1)} %get-tuple-element.68) | copy-start | bytes 2359300
Sparse Core Ops, SparseCore 0:
  10.1 144.1 all-gather.1
  385.5 93.2 reduce-scatter.2
  482.3 214.6 reduce-scatter.4

commit v2 on v0

v2 whole, which is shorter than its diff:
```python
import functools

import jax
import jax.numpy as jnp
from jax import lax
from jax.experimental import pallas as pl
from jax.experimental.pallas import tpu as pltpu
from jax.sharding import PartitionSpec as P

NORM_EPS = 1e-5
MASKED = -1e30
F32 = jnp.float32
BF16 = jnp.bfloat16
MESH = pl.DeviceIdType.MESH
DMA = pltpu.SemaphoreType.DMA
VMEM_LIMIT = 63 * 2 ** 20
RING = 4
ROWS = 16
PIECES = 4
HERE, NEXT, FAR, PREV = range(RING)
BY_RANK = (FAR, NEXT, PREV, HERE)
COLORS = range(2)
NT = (((1,), (1,)), ((), ()))
TN = (((0,), (0,)), ((), ()))


def go(place, distance):
    return (place + distance) % RING


def model_place():
    m = lax.axis_index('model')
    return m // 2, m % 2


def fsdp_place():
    f = lax.axis_index('fsdp')
    return f // RING, f % RING


def chip_targets():
    x, c = model_place()
    return [{'model': 2 * x + 1 - c}, {'model': 2 * go(x, NEXT) + c}, {'model': 2 * go(x, PREV) + c}]


def plane_targets():
    z, y = fsdp_place()
    return {'z': [{'fsdp': RING * go(z, d) + y} for d in (NEXT, PREV)],
            'y': [{'fsdp': RING * z + go(y, d)} for d in (NEXT, PREV)]}


def greet(targets):
    for target in targets:
        pl.semaphore_signal(pltpu.get_barrier_semaphore(), inc=1, device_id=target, device_id_type=MESH)


def met(targets):
    pl.semaphore_wait(pltpu.get_barrier_semaphore(), len(targets))


def chip_and_plane():
    plane = plane_targets()
    return chip_targets() + plane['z'] + plane['y']


def row_block(i, size, first=0):
    return pl.ds(pl.multiple_of(i * size + first, min(size, ROWS)), size)


def lane_block(i, size):
    return pl.ds(i * size if isinstance(i, int) else pl.multiple_of(i * size, size), size)


def row_loop(n_rows, fn, size=ROWS):
    def step(i, carry):
        fn(i)
        return carry
    lax.fori_loop(0, n_rows // size, step, None)


def row_sum(value):
    return jnp.sum(value, axis=-1, keepdims=True)


def row_mean(value):
    return jnp.mean(value, axis=-1, keepdims=True)


class Exchange:
    def __init__(self, send, recv):
        self.send, self.recv = send, recv

    def remote(self, i, src, dst, target):
        return pltpu.make_async_remote_copy(src_ref=src, dst_ref=dst, send_sem=self.send.at[i], recv_sem=self.recv.at[i],
                                            device_id=target, device_id_type=MESH)

    def landing(self):
        return [dst for _, dst, _ in self.copies()]

    def start(self, *which):
        table = self.copies()
        for i in which:
            self.remote(i, *table[i]).start()

    def arrived(self, *which):
        places, table = self.landing(), self.copies()
        for i in which:
            _, _, target = table[i]
            self.remote(i, places[i], places[i], target).wait_recv()

    def sent(self, *which):
        table = self.copies()
        for i in which or range(len(table)):
            self.remote(i, *table[i]).wait_send()


class Gather(Exchange):
    OTHER, UP, DOWN, PASS_UP, PASS_DOWN, PREV_OTHER, NEXT_OTHER, FAR_UP_OTHER, FAR_DOWN_OTHER = COPIES = range(9)

    def __init__(self, src, out, send, recv, local):
        super().__init__(send, recv)
        self.src, self.out, self.local = src, out, local
        self.x, self.c = model_place()
        self.pos, _ = src.shape
        self.half = self.pos // 2

    def block(self, distance, core):
        return self.out.at[row_block(2 * go(self.x, distance) + core, self.pos)]

    def part(self, distance, core, lower):
        place = 2 * go(self.x, distance) + core
        return self.out.at[row_block(2 * place + lower, self.half)]

    def copies(self):
        c = self.c
        other, nxt, prv = chip_targets()
        own = self.block(HERE, c)
        parts = [self.part(PREV, c, False), self.part(NEXT, c, True), self.block(PREV, c), self.block(NEXT, c),
                 self.part(FAR, c, False), self.part(FAR, c, True)]
        return [(self.src, own, other), (self.src, own, nxt), (self.src, own, prv)] + [
            (part, part, to) for part, to in zip(parts, (nxt, prv, other, other, other, other))]

    def landing(self):
        c, o = self.c, 1 - self.c
        return [self.block(HERE, o), self.block(PREV, c), self.block(NEXT, c), self.part(FAR, c, False),
                self.part(FAR, c, True), self.block(PREV, o), self.block(NEXT, o), self.part(FAR, o, False),
                self.part(FAR, o, True)]

    def own_copy(self):
        return pltpu.make_async_copy(self.src, self.block(HERE, self.c), self.local)

    def begin(self):
        if self.local is not None:
            self.own_copy().start()
        self.start(self.UP, self.DOWN, self.OTHER)

    def pass_near(self):
        self.arrived(self.UP)
        self.start(self.PASS_UP, self.PREV_OTHER)
        self.arrived(self.DOWN)
        self.start(self.PASS_DOWN, self.NEXT_OTHER)

    def pass_far(self):
        self.arrived(self.PASS_UP)
        self.start(self.FAR_UP_OTHER)
        self.arrived(self.PASS_DOWN)
        self.start(self.FAR_DOWN_OTHER)

    def complete(self):
        self.arrived(self.OTHER, self.PREV_OTHER, self.NEXT_OTHER, self.FAR_UP_OTHER, self.FAR_DOWN_OTHER)
        if self.local is not None:
            self.own_copy().wait()

    @classmethod
    def sems(cls, n):
        return [DMA((n, len(cls.COPIES))), DMA((n, len(cls.COPIES))), DMA((n,))]

    @classmethod
    def of(cls, i, src, out, sems, local=True):
        send, recv, local_sem = sems
        return cls(src, out, send.at[i], recv.at[i], local_sem.at[i] if local else None)


class RingGather(Exchange):
    UP, DOWN, PASS_UP, PASS_DOWN = COPIES = range(4)

    def __init__(self, src, at, targets, send, recv):
        super().__init__(send, recv)
        self.src, self.at, self.targets = src, at, targets
        rows, _ = src.shape
        self.upper, self.lower = row_block(0, rows // 2), row_block(1, rows // 2)

    def copies(self):
        nxt, prv = self.targets
        own, up, low = self.at(HERE), self.at(PREV).at[self.upper], self.at(NEXT).at[self.lower]
        return [(self.src, own, nxt), (self.src, own, prv), (up, up, nxt), (low, low, prv)]

    def landing(self):
        far = self.at(FAR)
        return [self.at(PREV), self.at(NEXT), far.at[self.upper], far.at[self.lower]]

    def begin(self):
        self.start(self.UP, self.DOWN)

    def pass_near(self):
        self.arrived(self.UP)
        self.start(self.PASS_UP)
        self.arrived(self.DOWN)
        self.start(self.PASS_DOWN)

    def far(self):
        self.arrived(self.PASS_UP, self.PASS_DOWN)


class WeightGather:
    def __init__(self, src, out, send, recv, local, first_row=0):
        self.src, self.out, self.local, self.first_row = src, out, local, first_row
        z, y = fsdp_place()
        self.place = RING * z + y
        self.rows, _ = src.shape
        half = self.rows // 2
        depth, _ = out.shape
        self.block = depth // RING ** 2
        targets = plane_targets()
        self.first, self.second = [], []
        for color, (one, two) in enumerate(('yz', 'zy')):
            part = src.at[row_block(color, half)]

            def at(d_one, d_two, one=one, color=color):
                dz, dy = (d_two, d_one) if one == 'y' else (d_one, d_two)
                first = (RING * go(z, dz) + go(y, dy)) * self.block + first_row + color * half
                return out.at[pl.ds(pl.multiple_of(first, ROWS), half)]
            self.first.append(RingGather(part, functools.partial(lambda at, d: at(d, HERE), at), targets[one],
                                         send.at[color, RING], recv.at[color, RING]))
            self.second.append([RingGather(at(d, HERE) if d else part, functools.partial(at, d), targets[two],
                                           send.at[color, d], recv.at[color, d]) for d in range(RING)])

    @staticmethod
    def sems(n):
        dims = (n, len(COLORS), RING + 1, len(RingGather.COPIES))
        return [DMA(dims), DMA(dims), DMA((n,))]

    @classmethod
    def of(cls, i, src, out, sems, local=True, first_row=0):
        send, recv, local_sem = sems
        return cls(src, out, send.at[i], recv.at[i], local_sem.at[i] if local else None, first_row)

    def own_rows(self):
        return pl.ds(pl.multiple_of(self.place * self.block + self.first_row, ROWS), self.rows)

    def own_copy(self):
        return pltpu.make_async_copy(self.src, self.out.at[self.own_rows()], self.local)

    def begin(self):
        if self.local is not None:
            self.own_copy().start()
        for ring in self.first:
            ring.begin()
        for rings in self.second:
            rings[HERE].begin()

    def pass_near(self):
        for one, two in zip(self.first, self.second):
            one.arrived(one.UP)
            one.start(one.PASS_UP)
            two[PREV].begin()
        for one, two in zip(self.first, self.second):
            one.arrived(one.DOWN)
            one.start(one.PASS_DOWN)
            two[NEXT].begin()
        self.pass_second(HERE)

    def pass_far(self):
        for one, two in zip(self.first, self.second):
            one.far()
            two[FAR].begin()

    def pass_second(self, d):
        for rings in self.second:
            rings[d].pass_near()

    def complete(self):
        for rings in self.second:
            for ring in rings:
                ring.far()
        if self.local is not None:
            self.own_copy().wait()

    def sent(self):
        for ring in self.first + sum(self.second, []):
            ring.sent()


class RingScatter(Exchange):
    FAR_UP, FAR_DOWN, UP_HI, DOWN_LO, UP_LO, DOWN_HI = COPIES = range(6)

    def __init__(self, mine, far, near, lo, hi, targets, send, recv):
        super().__init__(send, recv)
        self.mine, self.far, self.near, self.lo, self.hi, self.targets = mine, far, near, lo, hi, targets

    def copies(self):
        nxt, prv = self.targets
        far, up, down = (self.mine.at[BY_RANK.index(d)] for d in (FAR, NEXT, PREV))
        from_prv, from_nxt = self.near.at[0], self.near.at[1]
        lo, hi = self.lo, self.hi
        return [(far.at[lo], self.far.at[0], nxt), (far.at[hi], self.far.at[1], prv),
                (up.at[hi], from_prv.at[hi], nxt), (down.at[lo], from_nxt.at[lo], prv),
                (up.at[lo], from_prv.at[lo], nxt), (down.at[hi], from_nxt.at[hi], prv)]

    def begin(self):
        self.start(self.FAR_UP, self.FAR_DOWN, self.UP_HI, self.DOWN_LO)

    def add_far(self, add):
        up, down = (self.mine.at[BY_RANK.index(d)] for d in (NEXT, PREV))
        self.arrived(self.FAR_UP)
        add(up.at[self.lo], self.far.at[0])
        self.start(self.UP_LO)
        self.arrived(self.FAR_DOWN)
        add(down.at[self.hi], self.far.at[1])
        self.start(self.DOWN_HI)

    def arrive(self):
        self.arrived(self.UP_HI, self.DOWN_LO, self.UP_LO, self.DOWN_HI)

    def total(self, *at):
        return self.mine[(BY_RANK.index(HERE), *at)] + self.near[(0, *at)] + self.near[(1, *at)]


def add_rows(place, value):
    *outer, rows, _ = place.shape
    for at in [(i,) for i in range(*outer)] if outer else [()]:
        def add(i, at=at):
            place[(*at, row_block(i, ROWS))] += value[(*at, row_block(i, ROWS))]
        row_loop(rows, add)


class Scatter(Exchange):
    CHUNKS = 4

    def __init__(self, rows_of, weight, fetches, before, box, pair, mine, far, near, send, recv):
        super().__init__(send, recv)
        self.rows_of, self.weight, self.fetches, self.before = rows_of, weight, fetches, before
        self.box, self.pair, self.mine = box, pair, mine
        self.x, self.c = model_place()
        _, self.rows, self.width = mine.shape
        _, *ring_targets = chip_targets()
        half = self.width // 2
        rows = slice(None)
        ring_sems = (sem.at[pl.ds(RING, len(RingScatter.COPIES))] for sem in (send, recv))
        self.ring = RingScatter(mine, far, near, (rows, lane_block(0, half)), (rows, lane_block(1, half)), ring_targets,
                                *ring_sems)

    def copies(self):
        other, _, _ = chip_targets()
        return [(self.box.at[k], self.pair.at[k], other) for k in range(RING)]

    def pass_on(self, k):
        if self.before is not None:
            self.before.sent(k)
        chip = 2 * go(self.x, BY_RANK[k])
        left = jnp.concatenate([self.rows_of(chip + self.c), self.rows_of(chip + 1 - self.c)], axis=0)
        step = self.width // self.CHUNKS

        def chunk(i):
            if not k and self.fetches:
                for copy in self.fetches(i):
                    copy.wait()
            cols = lane_block(i, step)
            both = lax.dot_general(left, self.weight[cols, :], NT, preferred_element_type=F32)
            self.box[k, :, cols] = both[self.rows:]
            self.mine[k, :, cols] = both[:self.rows]
        row_loop(self.CHUNKS, chunk, 1)
        self.start(k)

    def pair_sum(self, k):
        self.arrived(k)
        add_rows(self.mine.at[k], self.pair.at[k])

    def send_near(self):
        far, up, down, here = range(RING)
        self.pass_on(far)
        self.pass_on(up)
        self.pair_sum(far)
        self.ring.start(RingScatter.FAR_UP, RingScatter.FAR_DOWN)
        self.pass_on(down)
        self.pair_sum(up)
        self.ring.start(RingScatter.UP_HI)
        self.pass_on(here)
        self.pair_sum(down)
        self.ring.start(RingScatter.DOWN_LO)

    def send_far(self):
        self.ring.add_far(add_rows)

    def arrive(self):
        self.pair_sum(BY_RANK.index(HERE))
        self.ring.arrive()

    def total(self, rows):
        return self.ring.total(rows)

    N_SCRATCH = 7

    @classmethod
    def scratch(cls, units, pos, width):
        sems = DMA((units, RING + len(RingScatter.COPIES)))
        return [pltpu.VMEM((RING, pos, width), F32), pltpu.VMEM((units, RING, pos, width), F32),
                pltpu.VMEM((units, RING, pos, width), F32), pltpu.VMEM((units, 2, pos, width // 2), F32),
                pltpu.VMEM((units, 2, pos, width), F32), sems, sems]

    @classmethod
    def all_of(cls, left, weight, fetches, scratch):
        box, *rest = scratch
        _, pos, _ = box.shape
        units, before = [], None
        n_seq, _, _ = left.shape
        for s in range(n_seq):
            def rows_of(place, s=s):
                return left[s, row_block(place, pos), :]
            before = cls(rows_of, weight, None if units else fetches, before, box, *(ref.at[s] for ref in rest))
            units.append(before)
        return units

    @staticmethod
    def all_sent(units):
        for unit in units:
            unit.ring.sent()
        unit.sent()


class GradScatter:
    N_SCRATCH = 9

    def __init__(self, part, out, mine1, far1, near1, mine2, far2, near2, send, recv, load):
        self.part, self.out, self.load, self.mine1, self.mine2 = part, out, load, mine1, mine2
        self.z, self.y = fsdp_place()
        rows, _ = out.shape
        self.half = rows // 2
        quarter = self.half // 2
        targets = plane_targets()
        self.one, self.two = [], []
        for color, (one, two) in enumerate(('yz', 'zy')):
            self.one.append(RingScatter(mine1.at[color], far1.at[color], near1.at[color], pl.ds(0, RING // 2),
                                        pl.ds(RING // 2, RING // 2), targets[one], send.at[color, 0], recv.at[color, 0]))
            self.two.append(RingScatter(mine2.at[color], far2.at[color], near2.at[color], row_block(0, quarter),
                                        row_block(1, quarter), targets[two], send.at[color, 1], recv.at[color, 1]))

    @staticmethod
    def scratch(rows, cols):
        half, n = rows // 2, len(COLORS)
        sems = DMA((n, 2, len(RingScatter.COPIES)))
        return [pltpu.VMEM((n, RING, RING, half, cols), F32), pltpu.VMEM((n, 2, RING // 2, half, cols), F32),
                pltpu.VMEM((n, 2, RING, half, cols), F32), pltpu.VMEM((n, RING, half, cols), F32),
                pltpu.VMEM((n, 2, half // 2, cols), F32), pltpu.VMEM((n, 2, half, cols), F32), sems, sems,
                DMA((n, RING, RING))]

    def loads(self):
        for color in COLORS:
            for k, d_one in enumerate(BY_RANK):
                for j, d_two in enumerate(BY_RANK):
                    dz, dy = (d_one, d_two) if color else (d_two, d_one)
                    place = RING * go(self.z, dz) + go(self.y, dy)
                    yield pltpu.make_async_copy(self.part.at[row_block(2 * place + color, self.half)],
                                                self.mine1.at[color, k, j], self.load.at[color, k, j])

    def fetch(self):
        for load in self.loads():
            load.start()

    def put(self, place, value):
        def rank(there, here):
            distance = (there + RING - here) % RING
            found = BY_RANK.index(HERE)
            for d in (NEXT, FAR, PREV):
                found = jnp.where(distance == d, BY_RANK.index(d), found)
            return found
        dz, dy = rank(place // RING, self.z), rank(place % RING, self.y)
        for color, at in enumerate(((dy, dz), (dz, dy))):
            self.mine1[(color, *at)] = value[color * self.half:(color + 1) * self.half]

    def begin(self):
        if self.part is not None:
            for load in self.loads():
                load.wait()
        for ring in self.one:
            ring.begin()

    def one_far(self):
        for ring in self.one:
            ring.add_far(add_rows)

    def one_done(self):
        for color, (one, two) in enumerate(zip(self.one, self.two)):
            one.arrive()
            for j in range(RING):
                def add(i, j=j):
                    rows = row_block(i, ROWS)
                    self.mine2[color, j, rows, :] = one.total(j, rows)
                row_loop(self.half, add)
            two.begin()

    def two_far(self):
        for ring in self.two:
            ring.add_far(add_rows)

    def two_done(self):
        for color, ring in enumerate(self.two):
            ring.arrive()

            def add(i):
                self.out[row_block(i, ROWS, color * self.half), :] = ring.total(row_block(i, ROWS))
            row_loop(self.half, add)

    def sent(self):
        for ring in self.one + self.two:
            ring.sent()


class GainSum:
    STAGES = 4

    def __init__(self, total, slots, send, recv):
        self.total, self.slots, self.send, self.recv = total, slots, send, recv
        (x, c), (z, y) = model_place(), fsdp_place()
        away = (NEXT, FAR, PREV)
        self.places = [c, x, y, z]
        self.targets = [[{'model': 2 * x + 1 - c}], [{'model': 2 * go(x, d) + c} for d in away],
                        [{'fsdp': RING * z + go(y, d)} for d in away], [{'fsdp': RING * go(z, d) + y} for d in away]]

    @classmethod
    def scratch(cls, *shape):
        dims = (cls.STAGES, RING - 1)
        return [pltpu.VMEM((cls.STAGES + 1, *shape), F32), pltpu.VMEM((*dims, *shape), F32), DMA(dims), DMA(dims)]

    def copies(self, t):
        return [pltpu.make_async_remote_copy(
            src_ref=self.total.at[t], dst_ref=self.slots.at[t, d], send_sem=self.send.at[t, d],
            recv_sem=self.recv.at[t, d], device_id=target, device_id_type=MESH)
            for d, target in enumerate(self.targets[t])]

    def start(self, t):
        for copy in self.copies(t):
            copy.start()

    def advance(self, t):
        others = len(self.targets[t])
        n = others + 1
        for copy in self.copies(t):
            copy.wait_recv()
        acc = None
        for i in range(n):
            term = self.total[t]
            for d in range(others):
                term = jnp.where((self.places[t] + others - d) % n == i, self.slots[t, d], term)
            acc = term if acc is None else acc + term
        self.total[t + 1] = acc
        if t + 1 < self.STAGES:
            self.start(t + 1)

    def sent(self):
        for t in range(self.STAGES):
            for copy in self.copies(t):
                copy.wait_send()


def norm_rows(x_f32, gain):
    return x_f32 * lax.rsqrt(row_mean(x_f32 * x_f32) + NORM_EPS) * gain


def norm_rows_back(x_f32, gain, cotangent):
    inv_rms = lax.rsqrt(row_mean(x_f32 * x_f32) + NORM_EPS)
    x_hat = x_f32 * inv_rms
    scaled = cotangent * gain
    return inv_rms * (scaled - x_hat * row_mean(scaled * x_hat)), cotangent * x_hat


def fold_row(row, out):
    rows, step = out.shape
    for i in range(rows):
        out[i:i + 1, :] = row[:, i * step:(i + 1) * step]


def unfold_row(rows_ref, out):
    rows, step = rows_ref.shape
    for i in range(rows):
        out[:, i * step:(i + 1) * step] = rows_ref[i:i + 1, :]


def rope_tables(cos_ref, sin_ref, cos_t, sin_t):
    cos, sin = cos_ref[...].T, sin_ref[...].T
    cos_t[...] = jnp.concatenate([cos, cos], axis=1)
    sin_t[...] = jnp.concatenate([-sin, sin], axis=1)


def spin(tensor, cos_t, sin_t):
    _, lanes = tensor.shape
    return tensor * cos_t + pltpu.roll(tensor, lanes // 2, 1) * sin_t


def probs(query, key, scale, first_row):
    scores = lax.dot_general(query, key, NT, preferred_element_type=F32) * scale
    rows, cols = (lax.broadcasted_iota(jnp.int32, scores.shape, dim) for dim in range(scores.ndim))
    scores = jnp.where(first_row + rows >= cols, scores, MASKED)
    expd = jnp.exp(scores - jnp.max(scores, axis=-1, keepdims=True))
    return expd / row_sum(expd)


def piece_of(refs, j, out):
    _, cols = out.shape
    step = cols // len(refs)
    for i, ref in enumerate(refs):
        out[:, lane_block(i, step)] = ref[:, lane_block(j, step)]


def fetch_weight(sources, w_vmem, sem):
    depth, _ = w_vmem.shape
    step = depth // Scatter.CHUNKS

    def chunk(i):
        rows, col, copies = row_block(i, step), 0, []
        for n, (ref, first, size) in enumerate(sources):
            copies.append(pltpu.make_async_copy(ref.at[rows, pl.ds(first, size)], w_vmem.at[rows, pl.ds(col, size)],
                                                sem.at[i, n]))
            col += size
        return copies
    for i in range(Scatter.CHUNKS):
        for copy in chunk(i):
            copy.start()
    return chunk


def piece_columns(pieces, first, size):
    return [(pieces.at[i], first, size) for i in range(PIECES)]


def early_rows(shard_rows):
    return 2 * shard_rows // 3


def first_kernel(heads, group, scale, x_ref, dy_ref, gain_ref, wqkv_src, wout_src, wg_ref, wu_ref, wd_ref, cos_ref, sin_ref,
                 h_out, dy_out, wqkv_out, wout_out, pieces_out, qkv_ref, attn_ref,
                 h_src, h_buf, w_buf, piece_src, cos_t, sin_t, flush, *sems):
    targets = chip_and_plane()
    greet(targets)
    n_seq, pos, _ = x_ref.shape
    seq, head_dim = cos_t.shape
    block = seq // 2
    _, cols = w_buf.shape
    x, c = model_place()
    mine = row_block(2 * x + c, pos)
    for s in range(n_seq):
        def norm(i, s=s):
            rows = row_block(i, ROWS)
            h_src[s, rows, :] = norm_rows(x_ref[s, rows, :].astype(F32), gain_ref[...]).astype(BF16)
        row_loop(pos, norm)
    g_sems, w_sems = sems[:3], sems[3:]
    w_qkv = WeightGather.of(0, wqkv_src, w_buf, w_sems[:3], local=False)
    w_out = WeightGather.of(0, wout_src, wout_out, w_sems[3:6])
    shard_rows, _ = wqkv_src.shape
    early = early_rows(shard_rows)
    piece = WeightGather.of(0, piece_src.at[pl.ds(0, early)], pieces_out.at[0], w_sems[6:])
    h0, h1 = (Gather.of(s, h_src.at[s], h_buf.at[s], g_sems, local=False) for s in range(n_seq))
    dy0, dy1 = (Gather.of(n_seq + s, dy_ref.at[s], dy_out.at[s], g_sems) for s in range(n_seq))
    met(targets)
    w_qkv.begin()
    h0.begin()
    h1.begin()
    piece_of((wg_ref, wu_ref, wd_ref), 0, piece_src)
    rope_tables(cos_ref, sin_ref, cos_t, sin_t)
    for s in range(n_seq):
        h_buf[s, mine, :] = h_src[s]
    w_buf[w_qkv.own_rows(), :] = wqkv_src[...]
    w_qkv.pass_near()
    h0.pass_near()
    w_qkv.pass_far()
    w_qkv.pass_second(PREV)
    w_qkv.pass_second(NEXT)
    w_out.begin()
    h1.pass_near()
    dy0.begin()
    w_qkv.pass_second(FAR)
    h0.pass_far()
    w_out.pass_near()
    w_qkv.complete()
    w_flush = pltpu.make_async_copy(w_buf, wqkv_out, flush.at[n_seq])
    w_flush.start()

    def lanes(i):
        return lane_block(i, head_dim)

    def project(s):
        def one_block(i):
            rows = row_block(i, block)
            qkv = jnp.dot(h_buf[s, rows, :], w_buf[...], preferred_element_type=F32)
            for j in range(cols // head_dim):
                one = qkv[:, j * head_dim:(j + 1) * head_dim]
                if j % (group + 2) <= group:
                    one = spin(one, cos_t[rows, :], sin_t[rows, :])
                qkv_ref[s, rows, lanes(j)] = one.astype(BF16)
        row_loop(seq, one_block, block)

    def attend(s):
        for g in range(heads // group):
            first = g * (group + 2)

            def head(j, first=first, g=g):
                for i in range(seq // block):
                    rows, keys = pl.ds(i * block, block), pl.ds(0, (i + 1) * block)
                    key, value = qkv_ref[s, keys, lanes(first + group)], qkv_ref[s, keys, lanes(first + group + 1)]
                    prob = probs(qkv_ref[s, rows, lanes(first + j)], key, scale, i * block)
                    attn_ref[s, rows, lanes(g * group + j)] = jnp.dot(
                        prob.astype(BF16), value, preferred_element_type=F32).astype(BF16)
            row_loop(group, head, 1)

    def h_flush(s):
        return pltpu.make_async_copy(h_buf.at[s], h_out.at[s], flush.at[s])

    h0.complete()
    h_flush(0).start()
    project(0)
    w_out.pass_far()
    h1.pass_far()
    dy1.begin()
    w_out.pass_second(PREV)
    w_out.pass_second(NEXT)
    piece.begin()
    attend(0)
    w_out.pass_second(FAR)
    dy0.pass_near()
    piece.pass_near()
    h1.complete()
    h_flush(1).start()
    project(1)
    piece.pass_far()
    piece.pass_second(PREV)
    dy0.pass_far()
    piece.pass_second(NEXT)
    dy1.pass_near()
    attend(1)
    piece.pass_second(FAR)
    dy1.pass_far()
    for each in (dy0, dy1, w_out, piece):
        each.complete()
    for each in (h0, h1, dy0, dy1, w_qkv, w_out, piece):
        each.sent()
    w_flush.wait()
    for s in range(n_seq):
        h_flush(s).wait()


def second_kernel(left, wout_hbm, base_ref, gain_ref, dy_hbm, wg_ref, wu_ref, wd_ref, pieces_in, mid_ref, h_out, act_ref,
                  dgu_ref, pieces_out, *scratch):
    targets = chip_and_plane()
    greet(targets)
    n_seq, pos, _ = base_ref.shape
    rs_scratch, scratch = scratch[:Scatter.N_SCRATCH], scratch[Scatter.N_SCRATCH:]
    wo_vmem, wo_sem, g_src, h_buf, dy_buf, dy_sem, w_bufs, w_sem, piece_src, flush, *scratch = scratch
    g_sems, p_sems = scratch[:3], scratch[3:]
    _, seq, _ = h_buf.shape
    block = seq // 2
    _, out_rows = wo_vmem.shape
    _, _, cols = w_bufs.shape
    step = cols // 3
    fetches = fetch_weight([(wout_hbm, 0, out_rows)], wo_vmem, wo_sem)
    shard_rows, _ = wg_ref.shape
    pieces = []
    for j in range(PIECES):
        piece_of((wg_ref, wu_ref, wd_ref), j, piece_src.at[j])
        early = 0 if j else early_rows(shard_rows)
        pieces.append(WeightGather.of(j, piece_src.at[j, pl.ds(early, shard_rows - early)], pieces_out.at[j], p_sems,
                                      first_row=early))
    p0, p1, p2, p3 = pieces
    x, c = model_place()
    mine = row_block(2 * x + c, pos)
    units = Scatter.all_of(left, wo_vmem, fetches, rs_scratch)
    u0, u1 = units
    h0, h1 = gathers = [Gather.of(s, g_src.at[s], h_buf.at[s], g_sems, local=False) for s in range(n_seq)]

    def settle(s, unit, gather):
        unit.arrive()

        def rows_fn(i):
            rows = row_block(i, ROWS)
            red = unit.total(rows).astype(BF16).astype(F32)
            mid = (base_ref[s, rows, :].astype(F32) + red).astype(BF16)
            mid_ref[s, rows, :] = mid
            g_src[s, rows, :] = norm_rows(mid.astype(F32), gain_ref[...]).astype(BF16)
        row_loop(pos, rows_fn)
        gather.begin()
        h_buf[s, mine, :] = g_src[s]

    def load_dy(s):
        return pltpu.make_async_copy(dy_hbm.at[s], dy_buf, dy_sem)

    def load_piece(t):
        return pltpu.make_async_copy(pieces_out.at[t % PIECES], w_bufs.at[t % 2], w_sem.at[t % 2])

    def h_flush(s):
        return pltpu.make_async_copy(h_buf.at[s], h_out.at[s], flush.at[s])

    def before_second():
        h1.pass_near()
        p3.pass_second(NEXT)
        p2.complete()

    def before_third():
        p3.pass_second(FAR)
        h1.pass_far()
        p3.complete()

    def before_next_sequence():
        load_dy(1).start()
        h1.complete()
        h_flush(1).start()
        load_dy(1).wait()

    def mlp(t):
        s, j, slot = t // PIECES, t % PIECES, t % 2
        for at, fn in {1: before_second, 2: before_third, PIECES: before_next_sequence}.items():
            pl.when(t == at)(fn)
        load_piece(t).wait()

        @pl.when(t + 1 < n_seq * PIECES)
        def _():
            load_piece(t + 1).start()

        def rows_fn(i):
            rows, there = row_block(i, block), row_block(i, block, s * seq)
            gate = jnp.dot(h_buf[s, rows, :], w_bufs[slot, :, :step], preferred_element_type=F32)
            up_proj = jnp.dot(h_buf[s, rows, :], w_bufs[slot, :, step:2 * step], preferred_element_type=F32)
            d_act = jnp.dot(dy_buf[rows, :], w_bufs[slot, :, 2 * step:],
                            preferred_element_type=F32).astype(BF16).astype(F32)
            sig_gate = jax.nn.sigmoid(gate)
            silu_gate = gate * sig_gate
            act_ref[there, lane_block(j, step)] = (silu_gate * up_proj).astype(BF16)
            dgu_ref[there, lane_block(2 * j, step)] = (
                d_act * up_proj * sig_gate * (1.0 + gate * (1.0 - sig_gate))).astype(BF16)
            dgu_ref[there, lane_block(2 * j + 1, step)] = (d_act * silu_gate).astype(BF16)
        row_loop(seq, rows_fn, block)

    load_dy(0).start()
    met(targets)
    p0.begin()
    p1.begin()
    u0.send_near()
    p0.pass_near()
    p1.pass_near()
    u0.send_far()
    p0.pass_far()
    p1.pass_far()
    p2.begin()
    p0.pass_second(PREV)
    p1.pass_second(PREV)
    u1.send_near()
    p0.pass_second(NEXT)
    p1.pass_second(NEXT)
    p0.pass_second(FAR)
    p2.pass_near()
    settle(0, u0, h0)
    u1.send_far()
    p1.pass_second(FAR)
    p2.pass_far()
    p3.begin()
    p2.pass_second(PREV)
    h0.pass_near()
    p2.pass_second(NEXT)
    p3.pass_near()
    p0.complete()
    load_piece(0).start()
    settle(1, u1, h1)
    h0.pass_far()
    p2.pass_second(FAR)
    p3.pass_far()
    p3.pass_second(PREV)
    p1.complete()
    h0.complete()
    h_flush(0).start()
    load_dy(0).wait()
    row_loop(n_seq * PIECES, mlp, 1)
    Scatter.all_sent(units)
    for each in gathers + pieces:
        each.sent()
    for s in range(n_seq):
        h_flush(s).wait()


def back_kernel(left, pieces, base_ref, mid_ref, gain_ref, res_ref, full_out, dgain_ref, *scratch):
    targets = chip_targets()
    greet(targets)
    n_seq, pos, _ = base_ref.shape
    rs_scratch, scratch = scratch[:Scatter.N_SCRATCH], scratch[Scatter.N_SCRATCH:]
    w_vmem, w_sem, g_src, sums, *sems = scratch
    _, depth = w_vmem.shape
    fetches = fetch_weight(piece_columns(pieces, 0, depth // PIECES), w_vmem, w_sem)
    units = Scatter.all_of(left, w_vmem, fetches, rs_scratch)
    u0, u1 = units
    g0, g1 = gathers = [Gather.of(s, g_src.at[s], full_out.at[s], sems) for s in range(n_seq)]
    sums[...] = jnp.zeros_like(sums)

    def settle(s, unit, gather):
        unit.arrive()

        def rows_fn(i):
            rows = row_block(i, ROWS)
            red = unit.total(rows).astype(BF16).astype(F32)
            d_norm, d_gain = norm_rows_back(mid_ref[s, rows, :].astype(F32), gain_ref[...], red)
            out = (base_ref[s, rows, :].astype(F32) + d_norm).astype(BF16)
            sums[...] += d_gain
            res_ref[s, rows, :] = out
            g_src[s, rows, :] = out
        row_loop(pos, rows_fn)
        gather.begin()

    met(targets)
    u0.send_near()
    u0.send_far()
    u1.send_near()
    settle(0, u0, g0)
    u1.send_far()
    g0.pass_near()
    settle(1, u1, g1)
    g0.pass_far()
    g1.pass_near()
    g1.pass_far()
    fold_row(jnp.sum(sums[...], axis=0, keepdims=True), dgain_ref)
    for gather in gathers:
        gather.complete()
    Scatter.all_sent(units)
    for gather in gathers:
        gather.sent()


def attn_back_kernel(heads, group, scale, dm_hbm, wo_hbm, h_hbm, left, pieces, rope_cos, rope_sin, qkv_ref, attn_ref, mid_ref,
                     dqkv_ref, dwqkv_out, y_ref, dwout_ref, *scratch):
    targets = chip_and_plane()
    greet(targets)
    _, pos, width = mid_ref.shape
    half_dim, seq = rope_cos.shape
    head_dim = 2 * half_dim
    block = seq // 2
    rs_scratch, scratch = scratch[:Scatter.N_SCRATCH], scratch[Scatter.N_SCRATCH:]
    grads = GradScatter(None, dwout_ref, *scratch[:GradScatter.N_SCRATCH])
    (wd_vmem, wd_sem, dm_ref, wo_ref, in_sem, h_buf, h_sem, dw_buf, dw_sem, do_ref, dk_ref, dv_ref, cos_ref,
     sin_ref) = scratch[GradScatter.N_SCRATCH:]
    _, ff = wd_vmem.shape
    piece_cols = ff // PIECES
    fetches = fetch_weight(piece_columns(pieces, 2 * piece_cols, piece_cols), wd_vmem, wd_sem)
    dm_copy = pltpu.make_async_copy(dm_hbm, dm_ref, in_sem.at[0])
    wo_copy = pltpu.make_async_copy(wo_hbm, wo_ref, in_sem.at[1])
    dm_copy.start()
    wo_copy.start()
    _, _, h_cols = h_buf.shape
    n_blocks = width // h_cols

    def h_copy(i):
        return pltpu.make_async_copy(h_hbm.at[:, lane_block(i, h_cols)], h_buf.at[i % 2], h_sem.at[i % 2])

    def dw_copy(i):
        return pltpu.make_async_copy(dw_buf.at[i % 2], dwqkv_out.at[row_block(i, h_cols)], dw_sem.at[i % 2])
    h_copy(0).start()
    rope_tables(rope_cos, rope_sin, cos_ref, sin_ref)
    units = Scatter.all_of(left, wd_vmem, fetches, rs_scratch)
    u0, u1 = units

    def settle(s, unit):
        unit.arrive()

        def rows_fn(i):
            rows = row_block(i, ROWS)
            red = unit.total(rows).astype(BF16).astype(F32)
            y_ref[s, rows, :] = (mid_ref[s, rows, :].astype(F32) + red).astype(BF16)
        row_loop(pos, rows_fn)

    def out_grads():
        shard, _ = dwout_ref.shape

        def two_places(i):
            both = lax.dot_general(dm_ref[:, lane_block(i, 2 * shard)], attn_ref[...], TN, preferred_element_type=F32)
            grads.put(2 * i, both[:shard])
            grads.put(2 * i + 1, both[shard:])
        row_loop(width, two_places, 2 * shard)

    def lanes(i):
        return lane_block(i, head_dim)

    def attention(s):
        base = s * seq

        def project(i):
            do_ref[row_block(i, block), :] = jnp.dot(dm_ref[row_block(i, block, base), :], wo_ref[...],
                                                     preferred_element_type=F32).astype(BF16)
        row_loop(seq, project, block)
        for g in range(heads // group):
            first = g * (group + 2)
            dk_ref[...] = jnp.zeros_like(dk_ref)
            dv_ref[...] = jnp.zeros_like(dv_ref)
            for i in range(seq // block):
                rows, keys = pl.ds(i * block, block), pl.ds(0, (i + 1) * block)
                g_rows, g_keys = pl.ds(base + i * block, block), pl.ds(base, (i + 1) * block)
                key, value = qkv_ref[g_keys, lanes(first + group)], qkv_ref[g_keys, lanes(first + group + 1)]

                def head(j, rows=rows, keys=keys, g_rows=g_rows, key=key, value=value, first=first, g=g, i=i):
                    query = qkv_ref[g_rows, lanes(first + j)]
                    d_out = do_ref[rows, lanes(g * group + j)]
                    prob = probs(query, key, scale, i * block)
                    d_prob = lax.dot_general(d_out, value, NT, preferred_element_type=F32)
                    d_scores = (prob * (d_prob - row_sum(d_prob * prob)) * scale).astype(BF16)
                    d_query = jnp.dot(d_scores, key, preferred_element_type=F32)
                    dqkv_ref[g_rows, lanes(first + j)] = spin(d_query, cos_ref[rows, :], -sin_ref[rows, :]).astype(BF16)
                    dk_ref[keys, :] += lax.dot_general(d_scores, query, TN, preferred_element_type=F32)
                    dv_ref[keys, :] += lax.dot_general(prob.astype(BF16), d_out, TN, preferred_element_type=F32)
                row_loop(group, head, 1)
            every = pl.ds(base, seq)
            dqkv_ref[every, lanes(first + group)] = spin(dk_ref[...], cos_ref[...], -sin_ref[...]).astype(BF16)
            dqkv_ref[every, lanes(first + group + 1)] = dv_ref[...].astype(BF16)

    def qkv_grads():
        def one_block(i):
            @pl.when(i + 1 < n_blocks)
            def _():
                h_copy(i + 1).start()
            h_copy(i).wait()

            @pl.when(i >= 2)
            def _():
                dw_copy(i - 2).wait()
            dw_buf[i % 2] = lax.dot_general(h_buf[i % 2], dqkv_ref[...], TN, preferred_element_type=F32)
            dw_copy(i).start()
        row_loop(n_blocks, one_block, 1)

    met(targets)
    u0.send_near()
    dm_copy.wait()
    out_grads()
    grads.begin()
    u0.send_far()
    u1.send_near()
    wo_copy.wait()
    attention(0)
    u1.send_far()
    grads.one_far()
    settle(0, u0)
    attention(1)
    grads.one_done()
    qkv_grads()
    settle(1, u1)
    grads.two_far()
    grads.two_done()
    for i in (n_blocks - 2, n_blocks - 1):
        dw_copy(i).wait()
    Scatter.all_sent(units)
    grads.sent()


def leave_kernel(left, w_hbm, base_ref, x_ref, gain_ref, grad_hbm, dgm_ref, res_ref, grad_ref, ga_ref, gm_ref, *scratch):
    _, pos, _ = base_ref.shape
    rs_scratch, scratch = scratch[:Scatter.N_SCRATCH], scratch[Scatter.N_SCRATCH:]
    grads = GradScatter(grad_hbm, grad_ref, *scratch[:GradScatter.N_SCRATCH])
    w_vmem, w_sem, sums, *gain_scratch = scratch[GradScatter.N_SCRATCH:]
    gains = GainSum(*gain_scratch)
    targets = sum(gains.targets, [])
    greet(targets)
    grads.fetch()
    _, depth = w_vmem.shape
    fetches = fetch_weight([(w_hbm, 0, depth)], w_vmem, w_sem)
    sums[...] = jnp.zeros_like(sums)
    units = Scatter.all_of(left, w_vmem, fetches, rs_scratch)
    u0, u1 = units

    def settle(s, unit):
        unit.arrive()

        def rows_fn(i):
            rows = row_block(i, ROWS)
            red = unit.total(rows).astype(BF16).astype(F32)
            red, d_gain = norm_rows_back(x_ref[s, rows, :].astype(F32), gain_ref[...], red)
            sums[...] += d_gain
            res_ref[s, rows, :] = (base_ref[s, rows, :].astype(F32) + red).astype(BF16)
        row_loop(pos, rows_fn)

    met(targets)
    grads.begin()
    u0.send_near()
    u0.send_far()
    grads.one_far()
    u1.send_near()
    u1.send_far()
    settle(0, u0)
    grads.one_done()
    settle(1, u1)
    rows, _ = dgm_ref.shape
    start, end = gains.total.at[0], gains.total.at[gains.STAGES]
    start[rows:, :] = dgm_ref[...]
    fold_row(jnp.sum(sums[...], axis=0, keepdims=True), start.at[pl.ds(0, rows)])
    gains.start(0)
    grads.two_far()
    for t in range(gains.STAGES):
        gains.advance(t)
    grads.two_done()
    unfold_row(end.at[pl.ds(0, rows)], ga_ref)
    unfold_row(end.at[pl.ds(rows, rows)], gm_ref)
    gains.sent()
    Scatter.all_sent(units)
    grads.sent()


def grad_kernel(h_ref, dy_ref, dgu_ref, act_ref, out_ref):
    _, cols = dgu_ref.shape
    out_ref[:, :cols] = lax.dot_general(h_ref[...], dgu_ref[...], TN, preferred_element_type=F32)
    out_ref[:, cols:] = lax.dot_general(dy_ref[...], act_ref[...], TN, preferred_element_type=F32)


def solution(mesh):
    act_spec = P('fsdp', 'model', None)
    rows_spec = P('fsdp', 'model')
    cols_spec = P('model', 'fsdp')

    def device_fn(x_loc, dy_loc, gain_attn, gain_mlp, wqkv_sh, wout_sh, wgate_sh, wup_sh, wdown_sh, rope_cos, rope_sin):
        n_seq, pos, width = x_loc.shape
        seq, half_dim = rope_cos.shape
        tokens = n_seq * seq
        head_dim = 2 * half_dim
        shard_rows, qkv_cols = wqkv_sh.shape
        out_rows, _ = wout_sh.shape
        ff, _ = wdown_sh.shape
        heads = out_rows // head_dim
        group = heads // ((qkv_cols - out_rows) // head_dim // 2)
        scale = head_dim ** -0.5
        gain_a, gain_m = gain_attn[None], gain_mlp[None]
        wout_t, wdown_t, cos_t, sin_t = wout_sh.T, wdown_sh.T, rope_cos.T, rope_sin.T
        piece_cols = 3 * ff // PIECES
        fold = 8

        vmem = pl.BlockSpec(memory_space=pltpu.VMEM)
        hbm = pl.BlockSpec(memory_space=pl.ANY)

        def shape(*dims, dtype=BF16):
            return jax.ShapeDtypeStruct(dims, dtype)

        def buf(*dims, dtype=BF16):
            return pltpu.VMEM(dims, dtype)

        def dma(*dims):
            return DMA(dims)

        def call(kernel, name, cid, us, ins, outs, scratch, args, aliases={}):
            spaces = {'V': vmem, 'H': hbm}
            shapes = tuple(out for _, out in outs)
            return pl.pallas_call(
                kernel, out_shape=shapes, in_specs=[spaces[i] for i in ins], out_specs=tuple(spaces[o] for o, _ in outs),
                scratch_shapes=scratch, name=name, input_output_aliases=aliases,
                cost_estimate=pl.CostEstimate(flops=us * 10 ** 9, bytes_accessed=10 ** 7, transcendentals=0),
                compiler_params=pltpu.CompilerParams(collective_id=cid, has_side_effects=True,
                                                     vmem_limit_bytes=VMEM_LIMIT))(*args)

        local, full = shape(n_seq, pos, width), shape(n_seq, seq, width)
        row_t, table = buf(ROWS, width, dtype=F32), buf(seq, head_dim, dtype=F32)
        shards = [wgate_sh, wup_sh, wdown_t]
        first, second, back, attn_back, leave = range(5)

        h_full, dy_full, w_qkv, w_out_t, pieces, qkv, attn = call(
            functools.partial(first_kernel, heads, group, scale), 'first', first, 50, 'V' * 10,
            [('H', full), ('H', full), ('H', shape(width, qkv_cols)), ('H', shape(width, out_rows)),
             ('H', shape(PIECES, width, piece_cols)), ('V', shape(n_seq, seq, qkv_cols)),
             ('V', shape(n_seq, seq, out_rows))],
            [buf(n_seq, pos, width), buf(n_seq, seq, width), buf(width, qkv_cols), buf(shard_rows, piece_cols), table,
             table, dma(n_seq + 1)] + Gather.sems(2 * n_seq) + 3 * WeightGather.sems(1),
            [x_loc, dy_loc, gain_a, wqkv_sh, wout_t] + shards + [cos_t, sin_t])

        mid, h_mlp, act, d_gu, pieces = call(
            second_kernel, 'second', second, 100, 'VHVVHVVVH',
            [('V', local), ('H', full), ('V', shape(tokens, ff)), ('V', shape(tokens, 2 * ff)),
             ('H', shape(PIECES, width, piece_cols))],
            Scatter.scratch(n_seq, pos, width)
            + [buf(width, out_rows), dma(Scatter.CHUNKS, 1), buf(n_seq, pos, width), buf(n_seq, seq, width),
               buf(seq, width), DMA, buf(2, width, piece_cols), dma(2), buf(PIECES, shard_rows, piece_cols), dma(n_seq)]
            + Gather.sems(n_seq) + WeightGather.sems(PIECES),
            [attn, w_out_t, x_loc, gain_m, dy_full] + shards + [pieces], aliases={8: 4})

        def whole(*dims):
            return pl.BlockSpec(dims, lambda i: (0,) * len(dims))

        block = width // 6

        def columns(rows):
            return pl.BlockSpec((rows, block), lambda i: (0, i))

        dw_mlp = pl.pallas_call(
            grad_kernel, grid=(width // block,), out_shape=shape(width, 3 * ff, dtype=F32),
            in_specs=[columns(tokens), columns(tokens), whole(tokens, 2 * ff), whole(tokens, ff)],
            out_specs=pl.BlockSpec((block, 3 * ff), lambda i: (i, 0)), name='grad_mlp',
            compiler_params=pltpu.CompilerParams(vmem_limit_bytes=VMEM_LIMIT),
        )(h_mlp.reshape(tokens, width), dy_full.reshape(tokens, width), d_gu, act)
        rs_mlp = lax.psum_scatter(dw_mlp, 'fsdp', scatter_dimension=0, tiled=True)
        d_gu, dw_mlp = lax.optimization_barrier((d_gu, dw_mlp))

        d_mid, d_mid_full, dgain_mlp = call(
            back_kernel, 'back', back, 90, 'VHVVV',
            [('V', local), ('H', full), ('V', shape(fold, width // fold, dtype=F32))],
            Scatter.scratch(n_seq, pos, width)
            + [buf(width, 2 * ff), dma(Scatter.CHUNKS, PIECES), buf(n_seq, pos, width), row_t] + Gather.sems(n_seq),
            [d_gu.reshape(n_seq, seq, 2 * ff), pieces, dy_loc, mid, gain_m])

        d_qkv, dw_qkv, y, rs_out_t = call(
            functools.partial(attn_back_kernel, heads, group, scale), 'attn_back', attn_back, 60, 'HHHVHVVVVV',
            [('V', shape(tokens, qkv_cols)), ('H', shape(width, qkv_cols, dtype=F32)), ('V', local),
             ('V', shape(shard_rows, out_rows, dtype=F32))],
            Scatter.scratch(n_seq, pos, width) + GradScatter.scratch(shard_rows, out_rows)
            + [buf(width, ff), dma(Scatter.CHUNKS, PIECES), buf(tokens, width), buf(width, out_rows), dma(2),
               buf(2, tokens, block), dma(2), buf(2, block, qkv_cols, dtype=F32), dma(2), buf(seq, out_rows)] + 4 * [table],
            [d_mid_full.reshape(tokens, width), w_out_t, h_full.reshape(tokens, width), act.reshape(n_seq, seq, ff), pieces,
             cos_t, sin_t, qkv.reshape(tokens, qkv_cols), attn.reshape(tokens, out_rows), mid])

        gain_out = shape(1, width, dtype=F32)
        dx, rs_qkv, gain_attn_sum, gain_mlp_sum = call(
            leave_kernel, 'leave', leave, 60, 'VHVVVHV',
            [('V', local), ('V', shape(shard_rows, qkv_cols, dtype=F32)), ('V', gain_out), ('V', gain_out)],
            Scatter.scratch(n_seq, pos, width) + GradScatter.scratch(shard_rows, qkv_cols)
            + [buf(width, qkv_cols), dma(Scatter.CHUNKS, 1), row_t] + GainSum.scratch(2 * fold, width // fold),
            [d_qkv.reshape(n_seq, seq, qkv_cols), w_qkv, d_mid, x_loc, gain_a, dw_qkv, dgain_mlp])

        def spread(i):
            step = ff // PIECES
            return jnp.concatenate([rs_mlp[:, (2 * j + i) * step:(2 * j + i + 1) * step] for j in range(PIECES)], axis=1)

        return (y, dx, gain_attn_sum[0], gain_mlp_sum[0], rs_qkv, rs_out_t.T, spread(0), spread(1), rs_mlp[:, 2 * ff:].T)

    in_specs = (act_spec, act_spec, P(), P(), rows_spec, cols_spec, rows_spec, rows_spec, cols_spec, P(), P())
    out_specs = (act_spec, act_spec, P(), P(), rows_spec, cols_spec, rows_spec, rows_spec, cols_spec)
    return jax.shard_map(device_fn, mesh=mesh, in_specs=in_specs, out_specs=out_specs, check_vma=False)
```

time: 1440 us -> 502 us (0.35)
  waiting for transfers between devices: 1090 us -> 7.34 us
  Pallas kernels: 0 us -> 470 us
  matrix products: 212 us -> 0 us
  blocking collectives: 68.5 us -> 0 us
  other arithmetic: 29.2 us -> 1.36 us
    reduce_scatter x13 -> x1, waiting for transfers between devices: 628 us -> 7.32 us  [device_fn(): rs_mlp = lax.psum_scatter(dw_mlp, 'fsdp', scatter_dimension=0, tiled=True)]
    pallas_call x0 -> x6, Pallas kernels: none -> 470 us  [the longest x5 443 us: call(): pl.pallas_call(kernel, out_shape=shapes, in_specs=[spaces[i] for i in ins...]
    all_gather x13 -> x0, waiting for transfers between devices: 454 us -> none  [the longest x8 201 us: gather_seq(): return lax.all_gather(tensor, 'model', axis=1, tiled=True)]
    dot_general x42 -> x0, matrix products: 212 us -> none  [the longest x2 22.3 us: micro_step(): jnp.einsum('bsf,df->bsd', d_up, w_up_b, preferred_element_type=jnp.float32)]
    psum x1 -> x0, blocking collectives: 68.5 us -> none  [device_fn(): gain_grads = lax.psum((accum[0], accum[1]), ('fsdp', 'model'))]
  transfers between devices with their start and end apart: 26 -> 1, of which waited for: 25 -> 1; matrix products, arithmetic and copies ran while one was open for 12% -> 0% of each run, Pallas kernels for 0% -> 52%
where the time goes in v2:
time: 502 us; the launch traced here: 501 us
  Pallas kernels  470 us (94%)
  between operations  14.1 us (3%)
  local copies, waits for them, and re-layouts  8.19 us (2%)
  waiting for transfers between devices  7.34 us (1%)
    pallas_call x5, Pallas kernels, call(): pl.pallas_call(kernel, out_shape=shapes, in_specs=[spaces[i] for i in ins...  443 us
    pallas_call x1, Pallas kernels, device_fn(): pl.pallas_call(grad_kernel, grid=(width // block,), out_shape=shape(width...  27.2 us
  transfers between devices with their start and end apart: 1, of which 1 were waited for; matrix products, arithmetic and copies ran while one was open for 0% of the time, Pallas kernels for 52%

profile of v2, /device:TPU:1, one launch (start us, length us, event | category | flops | bytes accessed | tf_op | source)
XLA Modules:
  0.0 501.3 jit_solution(7125109685689165839)
XLA Ops:
  7.2 0.0 reduce-scatter.2.cloned.1.call-start
  7.2 67.7 %first.1 = (bf16[2,512,3072]{2,1,0:T(8,128)(2,1)}, bf16[2,512,3072]{2,1,0:T(8,128)(2,1)}, bf16[3072,640]{1,0:T(8,128)(2,1)}, bf16[3072,384]{1,0:T(8,128)(2,1)}, ...) custom-call(bf16[2,64,3072]{2,1,0:T(8,128)(2,1)} %x_ref.3, ...), custom_call_target="tpu_custom_call" | custom-call | flops 49999998976 | bytes 10000000 | tf_op jit(solution)/shard_map/first/pallas_call | solution.py:1149
  74.9 116.2 %second.1 = (bf16[2,64,3072]{2,1,0:T(8,128)(2,1)}, bf16[2,512,3072]{2,1,0:T(8,128)(2,1)}, bf16[1024,1024]{1,0:T(8,128)(2,1)}, bf16[1024,2048]{1,0:T(8,128)(2,1)}, bf16[4,3072,768]{2,1,0:T(8,128)(2,1)}) custom-call(bf16[2,512,384]{2,1,0:T(8,128)(2,1)} %get-tuple-element.33.left, ...), custom_call_target="tpu_custom_call", output_to_operand_aliasing={{4}: (8, {})} | custom-call | flops 99999997952 | bytes 10000000 | tf_op jit(solution)/shard_map/second/pallas_call | solution.py:1149
  191.1 27.2 %grad_mlp.1 = f32[3072,3072]{1,0:T(8,128)} custom-call(bf16[1024,3072]{1,0:T(8,128)(2,1)} %bitcast.21, bf16[1024,3072]{1,0:T(8,128)(2,1)} %bitcast.20, bf16[1024,2048]{1,0:T(8,128)(2,1)} %get-tuple-element.40.dgu_ref, bf16[1024,1024]{1,0:T(8,128)(2,1)} %get-tuple-element.39.act_ref), custom_call_target="tpu_custom_call" | custom-call | tf_op jit(solution)/shard_map/grad_mlp/pallas_call | solution.py:1188
  218.3 0.0 reduce-scatter.2.cloned.1.call-update
  218.4 96.2 %back.1 = (bf16[2,64,3072]{2,1,0:T(8,128)(2,1)}, bf16[2,512,3072]{2,1,0:T(8,128)(2,1)}, f32[8,384]{1,0:T(8,128)}) custom-call(bf16[2,512,2048]{2,1,0:T(8,128)(2,1)} %bitcast.22, bf16[4,3072,768]{2,1,0:T(8,128)(2,1)} %get-tuple-element.41.pieces, bf16[2,64,3072]{2,1,0:T(8,128)(2,1)} %base_ref.3, bf16[2,64,3072]{2,1,0:T(8,128)(2,1)} %get-tuple-element.42.mid_ref, ...), custom_call_target="tpu_custom_call" | custom-call | flops 89999998976 | bytes 10000000 | tf_op jit(solution)/shard_map/back/pallas_call | solution.py:1149
  314.6 81.3 %attn_back.1 = (bf16[1024,640]{1,0:T(8,128)(2,1)}, f32[3072,640]{1,0:T(8,128)}, bf16[2,64,3072]{2,1,0:T(8,128)(2,1)}, f32[192,384]{1,0:T(8,128)}) custom-call(bf16[1024,3072]{1,0:T(8,128)(2,1)} %bitcast.39, bf16[3072,384]{1,0:T(8,128)(2,1)} %get-tuple-element.34.wout_hbm.wo_hbm, bf16[1024,3072]{1,0:T(8,128)(2,1)} %bitcast.38, ...), custom_call_target="tpu_custom_call" | custom-call | flops 60000002048 | bytes 10000000 | tf_op jit(solution)/shard_map/attn_back/pallas_call | solution.py:1149
  395.9 81.6 %leave.1 = (bf16[2,64,3072]{2,1,0:T(8,128)(2,1)}, f32[192,640]{1,0:T(8,128)}, f32[1,3072]{1,0:T(1,128)}, f32[1,3072]{1,0:T(1,128)}) custom-call(bf16[2,512,640]{2,1,0:T(8,128)(2,1)} %bitcast.41, bf16[3072,640]{1,0:T(8,128)(2,1)} %get-tuple-element.48.w_hbm, bf16[2,64,3072]{2,1,0:T(8,128)(2,1)} %get-tuple-element.49.base_ref, bf16[2,64,3072]{2,1,0:T(8,128)(2,1)} %x_ref.3, ...), custom_call_target="tpu_custom_call" | custom-call | flops 60000002048 | bytes 10000000 | tf_op jit(solution)/shard_map/leave/pallas_call | solution.py:1149
  477.5 0.0 copy-start
  477.5 0.0 copy-start.1
  477.5 7.3 %reduce-scatter.2.cloned.1.call-done = f32[192,3072]{1,0:T(8,128)} async-done(((f32[3072,3072]{1,0:T(8,128)}), f32[192,3072]{1,0:T(8,128)}) %reduce-scatter.2.cloned.1.call-update) | async-done | bytes 2359312 | tf_op jit(solution)/shard_map/reduce_scatter | solution.py:1194
  484.8 1.6 fusion
  486.5 0.0 copy-start.5
  486.5 0.0 copy-start.4
  486.5 0.0 copy-start.2
  486.5 0.0 copy-start.3
  486.5 1.4 pad_maximum_fusion
  487.9 2.1 slice_bitcast_fusion
  489.9 0.0 copy-done
  490.0 0.9 copy.28
  490.8 0.0 copy-done.1
  490.8 0.9 copy.29
  491.7 0.0 copy-done.5
  491.7 0.6 copy.30
  492.3 0.0 copy-done.4
  492.3 0.6 copy.31
  492.9 0.0 copy-done.2
  492.9 0.8 copy.32
  493.7 0.0 copy-done.3
  493.7 0.7 copy.33
Async XLA Ops:
  7.2 477.6 %reduce-scatter.2.cloned.1.call-start = ((), (), s32[]{:S(2)}) async-start(), calls=%async_computation.1 | async-start | bytes 40108032 | tf_op jit(solution)/shard_map/reduce_scatter | solution.py:1194
  477.5 12.5 %copy-start = (bf16[2,64,3072]{2,1,0:T(8,128)(2,1)S(1)}, bf16[2,64,3072]{2,1,0:T(8,128)(2,1)}, u32[]{:S(2)}) copy-start(bf16[2,64,3072]{2,1,0:T(8,128)(2,1)} %get-tuple-element.76) | copy-start | bytes 2359300
  477.5 13.3 %copy-start.1 = (bf16[2,64,3072]{2,1,0:T(8,128)(2,1)S(1)}, bf16[2,64,3072]{2,1,0:T(8,128)(2,1)}, u32[]{:S(2)}) copy-start(bf16[2,64,3072]{2,1,0:T(8,128)(2,1)} %get-tuple-element.77) | copy-start | bytes 2359300
  486.5 5.3 %copy-start.5 = (f32[1,3072]{1,0:T(1,128)S(1)}, f32[1,3072]{1,0:T(1,128)}, u32[]{:S(2)}) copy-start(f32[1,3072]{1,0:T(1,128)} %get-tuple-element.53) | copy-start | bytes 36868
  486.5 5.9 %copy-start.4 = (f32[1,3072]{1,0:T(1,128)S(1)}, f32[1,3072]{1,0:T(1,128)}, u32[]{:S(2)}) copy-start(f32[1,3072]{1,0:T(1,128)} %get-tuple-element.54) | copy-start | bytes 36868
  486.5 6.4 %copy-start.2 = (f32[192,640]{1,0:T(8,128)S(1)}, f32[192,640]{1,0:T(8,128)}, u32[]{:S(2)}) copy-start(f32[192,640]{1,0:T(8,128)} %get-tuple-element.80) | copy-start | bytes 1474564
  486.5 7.2 %copy-start.3 = (f32[192,384]{1,0:T(8,128)S(1)}, f32[192,384]{1,0:T(8,128)}, u32[]{:S(2)}) copy-start(f32[192,384]{1,0:T(8,128)} %get-tuple-element.56) | copy-start | bytes 884740
Sparse Core Ops, SparseCore 0:
  218.5 266.2 reduce-scatter.1

commit v3 on v2

--- a/solution.py
+++ b/solution.py
@@ -376,18 +376,20 @@
         self.arrived(k)
         add_rows(self.mine.at[k], self.pair.at[k])
 
-    def send_near(self):
+    def send_near(self, meanwhile=None):
         far, up, down, here = range(RING)
         self.pass_on(far)
-        self.pass_on(up)
+        if meanwhile is not None:
+            meanwhile()
         self.pair_sum(far)
         self.ring.start(RingScatter.FAR_UP, RingScatter.FAR_DOWN)
+        self.pass_on(up)
         self.pass_on(down)
         self.pair_sum(up)
         self.ring.start(RingScatter.UP_HI)
-        self.pass_on(here)
         self.pair_sum(down)
         self.ring.start(RingScatter.DOWN_LO)
+        self.pass_on(here)
 
     def send_far(self):
         self.ring.add_far(add_rows)
@@ -629,17 +631,13 @@
     return chunk
 
 
-def piece_columns(pieces, first, size):
-    return [(pieces.at[i], first, size) for i in range(PIECES)]
-
-
 def early_rows(shard_rows):
-    return 2 * shard_rows // 3
-
-
-def first_kernel(heads, group, scale, x_ref, dy_ref, gain_ref, wqkv_src, wout_src, wg_ref, wu_ref, wd_ref, cos_ref, sin_ref,
-                 h_out, dy_out, wqkv_out, wout_out, pieces_out, qkv_ref, attn_ref,
-                 h_src, h_buf, w_buf, piece_src, cos_t, sin_t, flush, *sems):
+    return shard_rows // 3
+
+
+def first_kernel(heads, group, scale, x_ref, dy_ref, gain_ref, wqkv_src, wout_src, wd_src, cos_ref, sin_ref,
+                 h_out, dy_out, wqkv_out, wout_out, wdown_out, qkv_ref, attn_ref,
+                 h_src, h_buf, w_buf, cos_t, sin_t, flush, *sems):
     targets = chip_and_plane()
     greet(targets)
     n_seq, pos, _ = x_ref.shape
@@ -658,29 +656,34 @@
     w_out = WeightGather.of(0, wout_src, wout_out, w_sems[3:6])
     shard_rows, _ = wqkv_src.shape
     early = early_rows(shard_rows)
-    piece = WeightGather.of(0, piece_src.at[pl.ds(0, early)], pieces_out.at[0], w_sems[6:])
+    w_down = WeightGather.of(0, wd_src.at[pl.ds(0, early)], wdown_out, w_sems[6:])
     h0, h1 = (Gather.of(s, h_src.at[s], h_buf.at[s], g_sems, local=False) for s in range(n_seq))
     dy0, dy1 = (Gather.of(n_seq + s, dy_ref.at[s], dy_out.at[s], g_sems) for s in range(n_seq))
     met(targets)
     w_qkv.begin()
     h0.begin()
     h1.begin()
-    piece_of((wg_ref, wu_ref, wd_ref), 0, piece_src)
     rope_tables(cos_ref, sin_ref, cos_t, sin_t)
     for s in range(n_seq):
         h_buf[s, mine, :] = h_src[s]
     w_buf[w_qkv.own_rows(), :] = wqkv_src[...]
     w_qkv.pass_near()
+    w_out.begin()
+    w_qkv.pass_far()
     h0.pass_near()
-    w_qkv.pass_far()
     w_qkv.pass_second(PREV)
     w_qkv.pass_second(NEXT)
-    w_out.begin()
+    w_out.pass_near()
+    w_down.begin()
+    w_qkv.pass_second(FAR)
     h1.pass_near()
     dy0.begin()
-    w_qkv.pass_second(FAR)
+    dy1.begin()
+    w_out.pass_far()
     h0.pass_far()
-    w_out.pass_near()
+    w_down.pass_near()
+    w_out.pass_second(PREV)
+    w_out.pass_second(NEXT)
     w_qkv.complete()
     w_flush = pltpu.make_async_copy(w_buf, wqkv_out, flush.at[n_seq])
     w_flush.start()
@@ -718,63 +721,60 @@
     h0.complete()
     h_flush(0).start()
     project(0)
-    w_out.pass_far()
+    w_down.pass_far()
+    w_out.pass_second(FAR)
     h1.pass_far()
-    dy1.begin()
-    w_out.pass_second(PREV)
-    w_out.pass_second(NEXT)
-    piece.begin()
     attend(0)
-    w_out.pass_second(FAR)
-    dy0.pass_near()
-    piece.pass_near()
+    w_down.pass_second(PREV)
+    w_down.pass_second(NEXT)
     h1.complete()
     h_flush(1).start()
     project(1)
-    piece.pass_far()
-    piece.pass_second(PREV)
+    dy0.pass_near()
+    w_down.pass_second(FAR)
+    attend(1)
     dy0.pass_far()
-    piece.pass_second(NEXT)
     dy1.pass_near()
-    attend(1)
-    piece.pass_second(FAR)
     dy1.pass_far()
-    for each in (dy0, dy1, w_out, piece):
+    for each in (dy0, dy1, w_out, w_down):
         each.complete()
-    for each in (h0, h1, dy0, dy1, w_qkv, w_out, piece):
+    for each in (h0, h1, dy0, dy1, w_qkv, w_out, w_down):
         each.sent()
     w_flush.wait()
     for s in range(n_seq):
         h_flush(s).wait()
 
 
-def second_kernel(left, wout_hbm, base_ref, gain_ref, dy_hbm, wg_ref, wu_ref, wd_ref, pieces_in, mid_ref, h_out, act_ref,
-                  dgu_ref, pieces_out, *scratch):
+def second_kernel(left, wout_hbm, base_ref, gain_ref, dy_hbm, wg_ref, wu_ref, wd_src, wdown_in, mid_ref, act_out, dgu_out,
+                  dw_out, pieces_out, wdown_out, *scratch):
     targets = chip_and_plane()
     greet(targets)
     n_seq, pos, _ = base_ref.shape
     rs_scratch, scratch = scratch[:Scatter.N_SCRATCH], scratch[Scatter.N_SCRATCH:]
-    wo_vmem, wo_sem, g_src, h_buf, dy_buf, dy_sem, w_bufs, w_sem, piece_src, flush, *scratch = scratch
+    (wo_vmem, wo_sem, g_src, h_buf, dy_buf, dy_sem, w_bufs, w_sem, piece_src, act_ref, dgu_ref, da_ref, dw_sem, flush,
+     *scratch) = scratch
+    _, _, stage, *_ = rs_scratch
     g_sems, p_sems = scratch[:3], scratch[3:]
-    _, seq, _ = h_buf.shape
+    tokens, _ = dy_buf.shape
+    seq = tokens // n_seq
     block = seq // 2
     _, out_rows = wo_vmem.shape
     _, _, cols = w_bufs.shape
-    step = cols // 3
+    step = cols // 2
     fetches = fetch_weight([(wout_hbm, 0, out_rows)], wo_vmem, wo_sem)
     shard_rows, _ = wg_ref.shape
-    pieces = []
-    for j in range(PIECES):
-        piece_of((wg_ref, wu_ref, wd_ref), j, piece_src.at[j])
-        early = 0 if j else early_rows(shard_rows)
-        pieces.append(WeightGather.of(j, piece_src.at[j, pl.ds(early, shard_rows - early)], pieces_out.at[j], p_sems,
-                                      first_row=early))
-    p0, p1, p2, p3 = pieces
+    early = early_rows(shard_rows)
+
+    def fill(j):
+        piece_of((wg_ref, wu_ref), j, piece_src.at[j])
+
+    p0, p1, p2, p3 = pieces = [WeightGather.of(j, piece_src.at[j], pieces_out.at[j], p_sems) for j in range(PIECES)]
+    w_down = WeightGather.of(PIECES, wd_src.at[pl.ds(early, shard_rows - early)], wdown_out, p_sems, first_row=early)
     x, c = model_place()
-    mine = row_block(2 * x + c, pos)
     units = Scatter.all_of(left, wo_vmem, fetches, rs_scratch)
     u0, u1 = units
-    h0, h1 = gathers = [Gather.of(s, g_src.at[s], h_buf.at[s], g_sems, local=False) for s in range(n_seq)]
+    h0, h1 = gathers = [Gather.of(s, g_src.at[s], h_buf.at[pl.ds(s * seq, seq)], g_sems, local=False)
+                        for s in range(n_seq)]
 
     def settle(s, unit, gather):
         unit.arrive()
@@ -787,49 +787,31 @@
             g_src[s, rows, :] = norm_rows(mid.astype(F32), gain_ref[...]).astype(BF16)
         row_loop(pos, rows_fn)
         gather.begin()
-        h_buf[s, mine, :] = g_src[s]
-
-    def load_dy(s):
-        return pltpu.make_async_copy(dy_hbm.at[s], dy_buf, dy_sem)
-
-    def load_piece(t):
-        return pltpu.make_async_copy(pieces_out.at[t % PIECES], w_bufs.at[t % 2], w_sem.at[t % 2])
-
-    def h_flush(s):
-        return pltpu.make_async_copy(h_buf.at[s], h_out.at[s], flush.at[s])
-
-    def before_second():
-        h1.pass_near()
-        p3.pass_second(NEXT)
-        p2.complete()
-
-    def before_third():
-        p3.pass_second(FAR)
-        h1.pass_far()
-        p3.complete()
-
-    def before_next_sequence():
-        load_dy(1).start()
-        h1.complete()
-        h_flush(1).start()
-        load_dy(1).wait()
-
-    def mlp(t):
-        s, j, slot = t // PIECES, t % PIECES, t % 2
-        for at, fn in {1: before_second, 2: before_third, PIECES: before_next_sequence}.items():
-            pl.when(t == at)(fn)
-        load_piece(t).wait()
-
-        @pl.when(t + 1 < n_seq * PIECES)
-        def _():
-            load_piece(t + 1).start()
-
+        h_buf[row_block(2 * x + c, pos, s * seq), :] = g_src[s]
+
+    dy_load = pltpu.make_async_copy(dy_hbm, dy_buf, dy_sem)
+    last = PIECES - 1
+
+    def load_down(half):
+        return pltpu.make_async_copy(wdown_out.at[:, lane_block(half, cols)], w_bufs.at[half], w_sem.at[half])
+
+    def load_piece(load):
+        piece = jnp.where(load == 2 * last, last, load % last)
+        return pltpu.make_async_copy(pieces_out.at[piece], w_bufs.at[load % 2], w_sem.at[load % 2])
+
+    def act_back(s, half):
         def rows_fn(i):
-            rows, there = row_block(i, block), row_block(i, block, s * seq)
-            gate = jnp.dot(h_buf[s, rows, :], w_bufs[slot, :, :step], preferred_element_type=F32)
-            up_proj = jnp.dot(h_buf[s, rows, :], w_bufs[slot, :, step:2 * step], preferred_element_type=F32)
-            d_act = jnp.dot(dy_buf[rows, :], w_bufs[slot, :, 2 * step:],
-                            preferred_element_type=F32).astype(BF16).astype(F32)
+            there = row_block(i, block, s * seq)
+            da_ref[there, lane_block(half, cols)] = jnp.dot(dy_buf[there, :], w_bufs[half],
+                                                            preferred_element_type=F32).astype(BF16)
+        row_loop(seq, rows_fn, block)
+
+    def mlp(s, j, load):
+        def rows_fn(i):
+            there = row_block(i, block, s * seq)
+            both = jnp.dot(h_buf[there, :], w_bufs[load % 2], preferred_element_type=F32)
+            gate, up_proj = both[:, :step], both[:, step:]
+            d_act = da_ref[there, lane_block(j, step)].astype(F32)
             sig_gate = jax.nn.sigmoid(gate)
             silu_gate = gate * sig_gate
             act_ref[there, lane_block(j, step)] = (silu_gate * up_proj).astype(BF16)
@@ -838,50 +820,124 @@
             dgu_ref[there, lane_block(2 * j + 1, step)] = (d_act * silu_gate).astype(BF16)
         row_loop(seq, rows_fn, block)
 
-    load_dy(0).start()
+    def all_but_last(load):
+        def ahead_of_second():
+            h1.pass_near()
+            p2.complete()
+            p3.pass_far()
+
+        def ahead_of_third():
+            h1.pass_far()
+            p3.pass_second(PREV)
+            p3.pass_second(NEXT)
+
+        def ahead_of_next_sequence():
+            h1.complete()
+            p3.pass_second(FAR)
+
+        for at, fn in {1: ahead_of_second, 2: ahead_of_third, last: ahead_of_next_sequence, 2 * last - 1: p3.complete}.items():
+            pl.when(load == at)(fn)
+        load_piece(load).wait()
+        load_piece(load + 1).start()
+        mlp(load // last, load % last, load)
+
+    _, kept_rows, _ = g_src.shape
+    col_step = RING * kept_rows
+    per_block = col_step // kept_rows
+    width, _ = wo_vmem.shape
+    _, cols_gu = dgu_ref.shape
+
+    def dw_copies(i):
+        return [pltpu.make_async_copy(stage.at[i % 2, k], dw_out.at[row_block(i * per_block + k, kept_rows)],
+                                      dw_sem.at[i % 2, k]) for k in range(per_block)]
+
+    def weight_grads(i):
+        slot = i % 2
+
+        @pl.when(i >= 2)
+        def _():
+            for copy in dw_copies(i - 2):
+                copy.wait()
+        half = cols_gu // 2
+        h_t, dy_t = h_buf[:, lane_block(i, col_step)], dy_buf[:, lane_block(i, col_step)]
+        for n, (left_cols, right) in enumerate(((h_t, dgu_ref[:, :half]), (h_t, dgu_ref[:, half:]), (dy_t, act_ref[...]))):
+            block_of = lax.dot_general(left_cols, right, TN, preferred_element_type=F32)
+            for k in range(per_block):
+                stage[slot, k, :, lane_block(n, half)] = block_of[k * kept_rows:(k + 1) * kept_rows]
+        for copy in dw_copies(i):
+            copy.start()
+
+    dy_load.start()
+
+    def fill_first():
+        for j in (0, 1):
+            fill(j)
+        w_down.begin()
+        p0.begin()
+
     met(targets)
-    p0.begin()
+    u0.send_near(fill_first)
+    for j in range(2, PIECES):
+        fill(j)
+    w_down.pass_near()
+    u0.send_far()
+    w_down.pass_far()
+    p0.pass_near()
+    w_down.pass_second(PREV)
+    w_down.pass_second(NEXT)
+    u1.send_near()
     p1.begin()
-    u0.send_near()
-    p0.pass_near()
+    w_down.pass_second(FAR)
+    p0.pass_far()
+    p0.pass_second(PREV)
+    settle(0, u0, h0)
+    p0.pass_second(NEXT)
     p1.pass_near()
-    u0.send_far()
-    p0.pass_far()
+    u1.send_far()
+    w_down.complete()
+    load_down(0).start()
+    load_down(1).start()
+    p0.pass_second(FAR)
     p1.pass_far()
     p2.begin()
-    p0.pass_second(PREV)
+    dy_load.wait()
+    load_down(0).wait()
+    act_back(0, 0)
     p1.pass_second(PREV)
-    u1.send_near()
-    p0.pass_second(NEXT)
+    act_back(1, 0)
     p1.pass_second(NEXT)
-    p0.pass_second(FAR)
     p2.pass_near()
-    settle(0, u0, h0)
-    u1.send_far()
+    h0.pass_near()
+    load_down(1).wait()
+    act_back(0, 1)
     p1.pass_second(FAR)
     p2.pass_far()
     p3.begin()
+    act_back(1, 1)
     p2.pass_second(PREV)
-    h0.pass_near()
-    p2.pass_second(NEXT)
-    p3.pass_near()
     p0.complete()
     load_piece(0).start()
     settle(1, u1, h1)
     h0.pass_far()
+    p2.pass_second(NEXT)
     p2.pass_second(FAR)
-    p3.pass_far()
-    p3.pass_second(PREV)
+    p3.pass_near()
     p1.complete()
     h0.complete()
-    h_flush(0).start()
-    load_dy(0).wait()
-    row_loop(n_seq * PIECES, mlp, 1)
+    row_loop(2 * last, all_but_last, 1)
+    load_piece(2 * last).wait()
+    mlp(0, last, 2 * last)
+    mlp(1, last, 2 * last)
+    flushes = [pltpu.make_async_copy(act_ref, act_out, flush.at[0]), pltpu.make_async_copy(dgu_ref, dgu_out, flush.at[1])]
+    for copy in flushes:
+        copy.start()
     Scatter.all_sent(units)
-    for each in gathers + pieces:
+    n_blocks = width // col_step
+    row_loop(n_blocks, weight_grads, 1)
+    for each in gathers + pieces + [w_down]:
         each.sent()
-    for s in range(n_seq):
-        h_flush(s).wait()
+    for copy in flushes + dw_copies(n_blocks - 2) + dw_copies(n_blocks - 1):
+        copy.wait()
 
 
 def back_kernel(left, pieces, base_ref, mid_ref, gain_ref, res_ref, full_out, dgain_ref, *scratch):
@@ -891,7 +947,7 @@
     rs_scratch, scratch = scratch[:Scatter.N_SCRATCH], scratch[Scatter.N_SCRATCH:]
     w_vmem, w_sem, g_src, sums, *sems = scratch
     _, depth = w_vmem.shape
-    fetches = fetch_weight(piece_columns(pieces, 0, depth // PIECES), w_vmem, w_sem)
+    fetches = fetch_weight([(pieces.at[j], 0, depth // PIECES) for j in range(PIECES)], w_vmem, w_sem)
     units = Scatter.all_of(left, w_vmem, fetches, rs_scratch)
     u0, u1 = units
     g0, g1 = gathers = [Gather.of(s, g_src.at[s], full_out.at[s], sems) for s in range(n_seq)]
@@ -930,7 +986,7 @@
         gather.sent()
 
 
-def attn_back_kernel(heads, group, scale, dm_hbm, wo_hbm, h_hbm, left, pieces, rope_cos, rope_sin, qkv_ref, attn_ref, mid_ref,
+def attn_back_kernel(heads, group, scale, dm_hbm, wo_hbm, h_hbm, left, wd_hbm, rope_cos, rope_sin, qkv_ref, attn_ref, mid_ref,
                      dqkv_ref, dwqkv_out, y_ref, dwout_ref, *scratch):
     targets = chip_and_plane()
     greet(targets)
@@ -943,8 +999,7 @@
     (wd_vmem, wd_sem, dm_ref, wo_ref, in_sem, h_buf, h_sem, dw_buf, dw_sem, do_ref, dk_ref, dv_ref, cos_ref,
      sin_ref) = scratch[GradScatter.N_SCRATCH:]
     _, ff = wd_vmem.shape
-    piece_cols = ff // PIECES
-    fetches = fetch_weight(piece_columns(pieces, 2 * piece_cols, piece_cols), wd_vmem, wd_sem)
+    fetches = fetch_weight([(wd_hbm, 0, ff)], wd_vmem, wd_sem)
     dm_copy = pltpu.make_async_copy(dm_hbm, dm_ref, in_sem.at[0])
     wo_copy = pltpu.make_async_copy(wo_hbm, wo_ref, in_sem.at[1])
     dm_copy.start()
@@ -1104,10 +1159,17 @@
     grads.sent()
 
 
-def grad_kernel(h_ref, dy_ref, dgu_ref, act_ref, out_ref):
-    _, cols = dgu_ref.shape
-    out_ref[:, :cols] = lax.dot_general(h_ref[...], dgu_ref[...], TN, preferred_element_type=F32)
-    out_ref[:, cols:] = lax.dot_general(dy_ref[...], act_ref[...], TN, preferred_element_type=F32)
+def outputs_kernel(grads_ref, *refs):
+    *refs, gate_ref, up_ref, down_ref = refs
+    n = len(refs) // 2
+    for src, dst in zip(refs[:n], refs[n:]):
+        dst[...] = src[...]
+    _, ff = gate_ref.shape
+    step = ff // PIECES
+    for j in range(PIECES):
+        gate_ref[:, lane_block(j, step)] = grads_ref[:, lane_block(2 * j, step)]
+        up_ref[:, lane_block(j, step)] = grads_ref[:, lane_block(2 * j + 1, step)]
+    down_ref[...] = grads_ref[:, lane_block(2, ff)]
 
 
 def solution(mesh):
@@ -1128,7 +1190,7 @@
         scale = head_dim ** -0.5
         gain_a, gain_m = gain_attn[None], gain_mlp[None]
         wout_t, wdown_t, cos_t, sin_t = wout_sh.T, wdown_sh.T, rope_cos.T, rope_sin.T
-        piece_cols = 3 * ff // PIECES
+        piece_cols = 2 * ff // PIECES
         fold = 8
 
         vmem = pl.BlockSpec(memory_space=pltpu.VMEM)
@@ -1155,42 +1217,29 @@
 
         local, full = shape(n_seq, pos, width), shape(n_seq, seq, width)
         row_t, table = buf(ROWS, width, dtype=F32), buf(seq, head_dim, dtype=F32)
-        shards = [wgate_sh, wup_sh, wdown_t]
         first, second, back, attn_back, leave = range(5)
 
-        h_full, dy_full, w_qkv, w_out_t, pieces, qkv, attn = call(
-            functools.partial(first_kernel, heads, group, scale), 'first', first, 50, 'V' * 10,
+        h_full, dy_full, w_qkv, w_out_t, w_down_t, qkv, attn = call(
+            functools.partial(first_kernel, heads, group, scale), 'first', first, 50, 'V' * 8,
             [('H', full), ('H', full), ('H', shape(width, qkv_cols)), ('H', shape(width, out_rows)),
-             ('H', shape(PIECES, width, piece_cols)), ('V', shape(n_seq, seq, qkv_cols)),
+             ('H', shape(width, ff)), ('V', shape(n_seq, seq, qkv_cols)),
              ('V', shape(n_seq, seq, out_rows))],
-            [buf(n_seq, pos, width), buf(n_seq, seq, width), buf(width, qkv_cols), buf(shard_rows, piece_cols), table,
+            [buf(n_seq, pos, width), buf(n_seq, seq, width), buf(width, qkv_cols), table,
              table, dma(n_seq + 1)] + Gather.sems(2 * n_seq) + 3 * WeightGather.sems(1),
-            [x_loc, dy_loc, gain_a, wqkv_sh, wout_t] + shards + [cos_t, sin_t])
-
-        mid, h_mlp, act, d_gu, pieces = call(
+            [x_loc, dy_loc, gain_a, wqkv_sh, wout_t, wdown_t, cos_t, sin_t])
+
+        mid, act, d_gu, dw_mlp, pieces, w_down_t = call(
             second_kernel, 'second', second, 100, 'VHVVHVVVH',
-            [('V', local), ('H', full), ('V', shape(tokens, ff)), ('V', shape(tokens, 2 * ff)),
-             ('H', shape(PIECES, width, piece_cols))],
+            [('V', local), ('H', shape(tokens, ff)), ('H', shape(tokens, 2 * ff)), ('H', shape(width, 3 * ff, dtype=F32)),
+             ('H', shape(PIECES, width, piece_cols)), ('H', shape(width, ff))],
             Scatter.scratch(n_seq, pos, width)
-            + [buf(width, out_rows), dma(Scatter.CHUNKS, 1), buf(n_seq, pos, width), buf(n_seq, seq, width),
-               buf(seq, width), DMA, buf(2, width, piece_cols), dma(2), buf(PIECES, shard_rows, piece_cols), dma(n_seq)]
-            + Gather.sems(n_seq) + WeightGather.sems(PIECES),
-            [attn, w_out_t, x_loc, gain_m, dy_full] + shards + [pieces], aliases={8: 4})
-
-        def whole(*dims):
-            return pl.BlockSpec(dims, lambda i: (0,) * len(dims))
+            + [buf(width, out_rows), dma(Scatter.CHUNKS, 1), buf(n_seq, pos, width), buf(tokens, width),
+               buf(tokens, width), DMA, buf(2, width, piece_cols), dma(2), buf(PIECES, shard_rows, piece_cols),
+               buf(tokens, ff), buf(tokens, 2 * ff), buf(tokens, ff), dma(2, RING), dma(2)]
+            + Gather.sems(n_seq) + WeightGather.sems(PIECES + 1),
+            [attn, w_out_t, x_loc, gain_m, dy_full.reshape(tokens, width), wgate_sh, wup_sh, wdown_t, w_down_t], aliases={8: 5})
 
         block = width // 6
-
-        def columns(rows):
-            return pl.BlockSpec((rows, block), lambda i: (0, i))
-
-        dw_mlp = pl.pallas_call(
-            grad_kernel, grid=(width // block,), out_shape=shape(width, 3 * ff, dtype=F32),
-            in_specs=[columns(tokens), columns(tokens), whole(tokens, 2 * ff), whole(tokens, ff)],
-            out_specs=pl.BlockSpec((block, 3 * ff), lambda i: (i, 0)), name='grad_mlp',
-            compiler_params=pltpu.CompilerParams(vmem_limit_bytes=VMEM_LIMIT),
-        )(h_mlp.reshape(tokens, width), dy_full.reshape(tokens, width), d_gu, act)
         rs_mlp = lax.psum_scatter(dw_mlp, 'fsdp', scatter_dimension=0, tiled=True)
         d_gu, dw_mlp = lax.optimization_barrier((d_gu, dw_mlp))
 
@@ -1206,9 +1255,9 @@
             [('V', shape(tokens, qkv_cols)), ('H', shape(width, qkv_cols, dtype=F32)), ('V', local),
              ('V', shape(shard_rows, out_rows, dtype=F32))],
             Scatter.scratch(n_seq, pos, width) + GradScatter.scratch(shard_rows, out_rows)
-            + [buf(width, ff), dma(Scatter.CHUNKS, PIECES), buf(tokens, width), buf(width, out_rows), dma(2),
+            + [buf(width, ff), dma(Scatter.CHUNKS, 1), buf(tokens, width), buf(width, out_rows), dma(2),
                buf(2, tokens, block), dma(2), buf(2, block, qkv_cols, dtype=F32), dma(2), buf(seq, out_rows)] + 4 * [table],
-            [d_mid_full.reshape(tokens, width), w_out_t, h_full.reshape(tokens, width), act.reshape(n_seq, seq, ff), pieces,
+            [d_mid_full.reshape(tokens, width), w_out_t, h_full.reshape(tokens, width), act.reshape(n_seq, seq, ff), w_down_t,
              cos_t, sin_t, qkv.reshape(tokens, qkv_cols), attn.reshape(tokens, out_rows), mid])
 
         gain_out = shape(1, width, dtype=F32)
@@ -1219,11 +1268,12 @@
             + [buf(width, qkv_cols), dma(Scatter.CHUNKS, 1), row_t] + GainSum.scratch(2 * fold, width // fold),
             [d_qkv.reshape(n_seq, seq, qkv_cols), w_qkv, d_mid, x_loc, gain_a, dw_qkv, dgain_mlp])
 
-        def spread(i):
-            step = ff // PIECES
-            return jnp.concatenate([rs_mlp[:, (2 * j + i) * step:(2 * j + i + 1) * step] for j in range(PIECES)], axis=1)
-
-        return (y, dx, gain_attn_sum[0], gain_mlp_sum[0], rs_qkv, rs_out_t.T, spread(0), spread(1), rs_mlp[:, 2 * ff:].T)
+        parts = (y, dx, gain_attn_sum, gain_mlp_sum, rs_qkv, rs_out_t)
+        outs = tuple(jax.ShapeDtypeStruct(part.shape, part.dtype) for part in parts) + (shape(shard_rows, ff, dtype=F32),) * 3
+        y, dx, gain_attn_sum, gain_mlp_sum, rs_qkv, rs_out_t, d_gate_w, d_up_w, d_down_t = pl.pallas_call(
+            outputs_kernel, out_shape=outs, in_specs=[vmem] * (len(parts) + 1), out_specs=(vmem,) * len(outs), name='outputs',
+            compiler_params=pltpu.CompilerParams(vmem_limit_bytes=VMEM_LIMIT))(rs_mlp, *parts)
+        return y, dx, gain_attn_sum[0], gain_mlp_sum[0], rs_qkv, rs_out_t.T, d_gate_w, d_up_w, d_down_t.T
 
     in_specs = (act_spec, act_spec, P(), P(), rows_spec, cols_spec, rows_spec, rows_spec, cols_spec, P(), P())
     out_specs = (act_spec, act_spec, P(), P(), rows_spec, cols_spec, rows_spec, rows_spec, cols_spec)

time: 502 us -> 485 us (0.966)
  local copies, waits for them, and re-layouts: 8.19 us -> 0 us
    pallas_call x1, Pallas kernels: 27.2 us -> 4.56 us  [device_fn(): pl.pallas_call(outputs_kernel, out_shape=outs, in_specs=[vmem] * (len(par...]
    pallas_call x5, Pallas kernels: 443 us -> 462 us  [call(): pl.pallas_call(kernel, out_shape=shapes, in_specs=[spaces[i] for i in ins...]
  transfers between devices with their start and end apart: 1 -> 1, of which waited for: 1 -> 1; matrix products, arithmetic and copies ran while one was open for 0% -> 0% of each run, Pallas kernels for 52% -> 54%
where the time goes in v3:
time: 485 us; the launch traced here: 484 us
  Pallas kernels  466 us (96%)
  between operations  14.1 us (3%)
    pallas_call x5, Pallas kernels, call(): pl.pallas_call(kernel, out_shape=shapes, in_specs=[spaces[i] for i in ins...  462 us
  transfers between devices with their start and end apart: 1, of which 1 were waited for; matrix products, arithmetic and copies ran while one was open for 0% of the time, Pallas kernels for 54%

profile of v3, /device:TPU:1, one launch (start us, length us, event | category | flops | bytes accessed | tf_op | source)
XLA Modules:
  0.0 484.4 jit_solution(4794739996922832542)
XLA Ops:
  7.2 0.0 reduce-scatter.2.cloned.1.call-start
  7.2 68.6 %first.1 = (bf16[2,512,3072]{2,1,0:T(8,128)(2,1)}, bf16[2,512,3072]{2,1,0:T(8,128)(2,1)}, bf16[3072,640]{1,0:T(8,128)(2,1)}, bf16[3072,384]{1,0:T(8,128)(2,1)}, ...) custom-call(bf16[2,64,3072]{2,1,0:T(8,128)(2,1)} %x_ref.3, ...), custom_call_target="tpu_custom_call" | custom-call | flops 49999998976 | bytes 10000000 | tf_op jit(solution)/shard_map/first/pallas_call | solution.py:1211
  75.8 130.0 %second.1 = (bf16[2,64,3072]{2,1,0:T(8,128)(2,1)}, bf16[1024,1024]{1,0:T(8,128)(2,1)}, bf16[1024,2048]{1,0:T(8,128)(2,1)}, f32[3072,3072]{1,0:T(8,128)}, bf16[4,...) custom-call(bf16[2,512,384]{2,1,0:T(8,128)(2,1)} %get-tuple-element.43.left, ...), custom_call_target="tpu_custom_call", output_to_operand_aliasing={{5}: (8, {})} | custom-call | flops 99999997952 | bytes 10000000 | tf_op jit(solution)/shard_map/second/pallas_call | solution.py:1211
  205.8 0.0 reduce-scatter.2.cloned.1.call-update
  205.8 95.2 %back.1 = (bf16[2,64,3072]{2,1,0:T(8,128)(2,1)}, bf16[2,512,3072]{2,1,0:T(8,128)(2,1)}, f32[8,384]{1,0:T(8,128)}) custom-call(bf16[2,512,2048]{2,1,0:T(8,128)(2,1)} %bitcast.36, bf16[4,3072,512]{2,1,0:T(8,128)(2,1)} %get-tuple-element.50.pieces, bf16[2,64,3072]{2,1,0:T(8,128)(2,1)} %base_ref.3, bf16[2,64,3072]{2,1,0:T(8,128)(2,1)} %get-tuple-element.51.mid_ref, ...), custom_call_target="tpu_custom_call" | custom-call | flops 89999998976 | bytes 10000000 | tf_op jit(solution)/shard_map/back/pallas_call | solution.py:1211
  301.0 83.5 %attn_back.1 = (bf16[1024,640]{1,0:T(8,128)(2,1)}, f32[3072,640]{1,0:T(8,128)}, bf16[2,64,3072]{2,1,0:T(8,128)(2,1)}, f32[192,384]{1,0:T(8,128)}) custom-call(bf16[1024,3072]{1,0:T(8,128)(2,1)} %bitcast.34, bf16[3072,384]{1,0:T(8,128)(2,1)} %get-tuple-element.44.wout_hbm.wo_hbm, bf16[1024,3072]{1,0:T(8,128)(2,1)} %bitcast.33, ...), custom_call_target="tpu_custom_call" | custom-call | flops 60000002048 | bytes 10000000 | tf_op jit(solution)/shard_map/attn_back/pallas_call | solution.py:1211
  384.5 84.4 %leave.1 = (bf16[2,64,3072]{2,1,0:T(8,128)(2,1)}, f32[192,640]{1,0:T(8,128)}, f32[1,3072]{1,0:T(1,128)}, f32[1,3072]{1,0:T(1,128)}) custom-call(bf16[2,512,640]{2,1,0:T(8,128)(2,1)} %bitcast.39, bf16[3072,640]{1,0:T(8,128)(2,1)} %get-tuple-element.59.w_hbm, bf16[2,64,3072]{2,1,0:T(8,128)(2,1)} %get-tuple-element.60.base_ref, bf16[2,64,3072]{2,1,0:T(8,128)(2,1)} %x_ref.3, ...), custom_call_target="tpu_custom_call" | custom-call | flops 60000002048 | bytes 10000000 | tf_op jit(solution)/shard_map/leave/pallas_call | solution.py:1211
  468.9 4.0 reduce-scatter.2.cloned.1.call-done.grads_ref
  473.0 4.6 outputs.1
Async XLA Ops:
  7.2 465.8 %reduce-scatter.2.cloned.1.call-start = ((), (), s32[]{:S(2)}) async-start(), calls=%async_computation.1 | async-start | bytes 40108032 | tf_op jit(solution)/shard_map/reduce_scatter | solution.py:1243
Sparse Core Ops, SparseCore 0:
  205.9 266.9 reduce-scatter.1

commit v4 on v3

--- a/solution.py
+++ b/solution.py
@@ -882,10 +882,10 @@
     w_down.pass_near()
     u0.send_far()
     w_down.pass_far()
-    p0.pass_near()
     w_down.pass_second(PREV)
     w_down.pass_second(NEXT)
     u1.send_near()
+    p0.pass_near()
     p1.begin()
     w_down.pass_second(FAR)
     p0.pass_far()

time: 485 us -> 490 us (1.010)
  Pallas kernels: 466 us -> 472 us
    pallas_call x5, Pallas kernels: 462 us -> 467 us  [call(): pl.pallas_call(kernel, out_shape=shapes, in_specs=[spaces[i] for i in ins...]
where the time goes in v4:
time: 490 us
  Pallas kernels  472 us (96%)
  between operations  14.1 us (3%)
    pallas_call x5, Pallas kernels, call(): pl.pallas_call(kernel, out_shape=shapes, in_specs=[spaces[i] for i in ins...  467 us
  transfers between devices with their start and end apart: 1, of which 1 were waited for; matrix products, arithmetic and copies ran while one was open for 0% of the time, Pallas kernels for 54%

profile of v4, /device:TPU:1, one launch (start us, length us, event | category | flops | bytes accessed | tf_op | source)
XLA Modules:
  0.0 489.9 jit_solution(7135621290357499471)
XLA Ops:
  7.2 0.0 reduce-scatter.2.cloned.1.call-start
  7.2 68.6 %first.1 = (bf16[2,512,3072]{2,1,0:T(8,128)(2,1)}, bf16[2,512,3072]{2,1,0:T(8,128)(2,1)}, bf16[3072,640]{1,0:T(8,128)(2,1)}, bf16[3072,384]{1,0:T(8,128)(2,1)}, ...) custom-call(bf16[2,64,3072]{2,1,0:T(8,128)(2,1)} %x_ref.3, ...), custom_call_target="tpu_custom_call" | custom-call | flops 49999998976 | bytes 10000000 | tf_op jit(solution)/shard_map/first/pallas_call | solution.py:1211
  75.8 135.3 %second.1 = (bf16[2,64,3072]{2,1,0:T(8,128)(2,1)}, bf16[1024,1024]{1,0:T(8,128)(2,1)}, bf16[1024,2048]{1,0:T(8,128)(2,1)}, f32[3072,3072]{1,0:T(8,128)}, bf16[4,...) custom-call(bf16[2,512,384]{2,1,0:T(8,128)(2,1)} %get-tuple-element.43.left, ...), custom_call_target="tpu_custom_call", output_to_operand_aliasing={{5}: (8, {})} | custom-call | flops 99999997952 | bytes 10000000 | tf_op jit(solution)/shard_map/second/pallas_call | solution.py:1211
  211.1 0.0 reduce-scatter.2.cloned.1.call-update
  211.1 95.1 %back.1 = (bf16[2,64,3072]{2,1,0:T(8,128)(2,1)}, bf16[2,512,3072]{2,1,0:T(8,128)(2,1)}, f32[8,384]{1,0:T(8,128)}) custom-call(bf16[2,512,2048]{2,1,0:T(8,128)(2,1)} %bitcast.36, bf16[4,3072,512]{2,1,0:T(8,128)(2,1)} %get-tuple-element.50.pieces, bf16[2,64,3072]{2,1,0:T(8,128)(2,1)} %base_ref.3, bf16[2,64,3072]{2,1,0:T(8,128)(2,1)} %get-tuple-element.51.mid_ref, ...), custom_call_target="tpu_custom_call" | custom-call | flops 89999998976 | bytes 10000000 | tf_op jit(solution)/shard_map/back/pallas_call | solution.py:1211
  306.2 83.8 %attn_back.1 = (bf16[1024,640]{1,0:T(8,128)(2,1)}, f32[3072,640]{1,0:T(8,128)}, bf16[2,64,3072]{2,1,0:T(8,128)(2,1)}, f32[192,384]{1,0:T(8,128)}) custom-call(bf16[1024,3072]{1,0:T(8,128)(2,1)} %bitcast.34, bf16[3072,384]{1,0:T(8,128)(2,1)} %get-tuple-element.44.wout_hbm.wo_hbm, bf16[1024,3072]{1,0:T(8,128)(2,1)} %bitcast.33, ...), custom_call_target="tpu_custom_call" | custom-call | flops 60000002048 | bytes 10000000 | tf_op jit(solution)/shard_map/attn_back/pallas_call | solution.py:1211
  390.0 84.2 %leave.1 = (bf16[2,64,3072]{2,1,0:T(8,128)(2,1)}, f32[192,640]{1,0:T(8,128)}, f32[1,3072]{1,0:T(1,128)}, f32[1,3072]{1,0:T(1,128)}) custom-call(bf16[2,512,640]{2,1,0:T(8,128)(2,1)} %bitcast.39, bf16[3072,640]{1,0:T(8,128)(2,1)} %get-tuple-element.59.w_hbm, bf16[2,64,3072]{2,1,0:T(8,128)(2,1)} %get-tuple-element.60.base_ref, bf16[2,64,3072]{2,1,0:T(8,128)(2,1)} %x_ref.3, ...), custom_call_target="tpu_custom_call" | custom-call | flops 60000002048 | bytes 10000000 | tf_op jit(solution)/shard_map/leave/pallas_call | solution.py:1211
  474.3 4.2 reduce-scatter.2.cloned.1.call-done.grads_ref
  478.5 4.6 outputs.1
Async XLA Ops:
  7.2 471.3 %reduce-scatter.2.cloned.1.call-start = ((), (), s32[]{:S(2)}) async-start(), calls=%async_computation.1 | async-start | bytes 40108032 | tf_op jit(solution)/shard_map/reduce_scatter | solution.py:1243
Sparse Core Ops, SparseCore 0:
  211.2 267.2 reduce-scatter.1
